TPU v7x, 64 devices: a 2x2x8 block of a 4x4x8 slice. The times are simulated.
64 devices in a mesh: batch: 4 (over x, y), dap: 16 (over z, core).
Axes of the slice: x: 2, y: 2, z: 8, core: 2. Of those that a mesh axis runs over, the one named last changes fastest.
The devices are a block of a 4x4x8 slice.
Arguments:
- pair_act: bfloat16 [1024, 256, 128], P(('batch', 'dap')), parts along dimension 0
- pair_mask: int32 [1024, 256], P(('batch', 'dap')), parts along dimension 0
- msa_act: bfloat16 [512, 1024, 256], P(None, ('batch', 'dap')), parts along dimension 1
- opm_norm: bfloat16 [2, 2, 256], replicated
- opm_w_in: bfloat16 [2, 256, 2, 32], replicated
- opm_b_in: bfloat16 [2, 2, 32], replicated
- opm_w_out: bfloat16 [2, 1024, 128], replicated
- opm_b_out: bfloat16 [2, 128], replicated
- tri_norm_in: bfloat16 [2, 2, 128], replicated
- tri_w_ab: bfloat16 [2, 128, 4, 128], replicated
- tri_b_ab: bfloat16 [2, 4, 128], replicated
- tri_w_gate: bfloat16 [2, 128, 128], replicated
- tri_b_gate: bfloat16 [2, 128], replicated
- tri_norm_out: bfloat16 [2, 2, 128], replicated
- tri_w_out: bfloat16 [2, 128, 128], replicated
- tri_b_out: bfloat16 [2, 128], replicated
Outputs:
- output: bfloat16 [1024, 256, 128], P(('batch', 'dap')), parts along dimension 0
There are 4 independent parts. A program takes and returns all parts, laid end to end along the dimension named above; an argument that names none is the same for every part.
All inputs are finite; a program needn't handle non-finite values.
Results may differ from a plain program's by a relative error of at most 0.0106456.
Values are sent between devices in bfloat16 or wider.
A program may use at most 768 MiB of HBM per device.

v0:
```python
import math
import jax
import jax.numpy as jnp
from jax import lax
from jax.sharding import PartitionSpec as P

LN_EPS = 1e-5
ROW_BLOCK = 8


def layer_norm(values, gain_scale, offset, norm_axis):
    x_f32 = values.astype(jnp.float32)
    mean_val = jnp.mean(x_f32, axis=norm_axis, keepdims=True)
    centered = x_f32 - mean_val
    var_val = jnp.mean(centered * centered, axis=norm_axis, keepdims=True)
    return (centered * lax.rsqrt(var_val + LN_EPS) * gain_scale + offset).astype(jnp.bfloat16)


def value_a15(value_a7, norm_w, w_in, b_in):
    normed = layer_norm(value_a7, norm_w[0].astype(jnp.float32), norm_w[1].astype(jnp.float32), -1)
    in_bias = b_in.astype(jnp.float32)
    left_proj = (jnp.einsum('sim,mc->sic', normed, w_in[:, 0, :], preferred_element_type=jnp.float32) + in_bias[0]).astype(jnp.bfloat16)
    right_proj = (jnp.einsum('sim,mc->sic', normed, w_in[:, 1, :], preferred_element_type=jnp.float32) + in_bias[1]).astype(jnp.bfloat16)
    return left_proj, right_proj


def outer_mean_rows(pair_act, left_proj, right_full, w_out, b_out):
    row_count, col_count, pair_dim = pair_act.shape
    value_a9 = left_proj.shape[0]
    opm_dim = left_proj.shape[2]
    row_blk = math.gcd(row_count, ROW_BLOCK)
    num_blocks = row_count // row_blk
    left_blocks = jnp.moveaxis(left_proj.reshape(value_a9, num_blocks, row_blk, opm_dim), 1, 0)
    pair_blocks = pair_act.reshape(num_blocks, row_blk, col_count, pair_dim)
    w_out_r = w_out.reshape(opm_dim, opm_dim, pair_dim)
    out_bias = b_out.astype(jnp.float32)

    def block_update(block_args):
        left_blk, pair_blk = block_args
        outer_prod = jnp.einsum('sic,sjd->icjd', left_blk, right_full, preferred_element_type=jnp.float32)
        outer_prod = (outer_prod / value_a9).astype(jnp.bfloat16)
        pair_upd = (jnp.einsum('icjd,cdz->ijz', outer_prod, w_out_r, preferred_element_type=jnp.float32) + out_bias).astype(jnp.bfloat16)
        return (pair_blk.astype(jnp.float32) + pair_upd.astype(jnp.float32)).astype(jnp.bfloat16)

    return lax.map(block_update, (left_blocks, pair_blocks)).reshape(row_count, col_count, pair_dim)


def gated_projection(normed, mask_f, w_pair, b_pair):
    projected = jnp.einsum('zqc,ikz->qcik', w_pair, normed, preferred_element_type=jnp.float32)
    projected = projected + b_pair.astype(jnp.float32)[:, :, None, None]
    return (mask_f[None] * jax.nn.sigmoid(projected[1]) * projected[0]).astype(jnp.bfloat16)


def triangle_finish(pair_act, normed, tri_prod, w_gate, b_gate, norm_out, w_out, b_out):
    gate_val = jax.nn.sigmoid(jnp.einsum('ikz,zy->iky', normed, w_gate, preferred_element_type=jnp.float32) + b_gate.astype(jnp.float32))
    out_gains = norm_out.astype(jnp.float32)[:, :, None, None]
    prod_norm = layer_norm(tri_prod, out_gains[0], out_gains[1], 0)
    pair_upd = (jnp.einsum('cij,cz->ijz', prod_norm, w_out, preferred_element_type=jnp.float32) + b_out.astype(jnp.float32)).astype(jnp.bfloat16)
    return (pair_act.astype(jnp.float32) + gate_val * pair_upd.astype(jnp.float32)).astype(jnp.bfloat16)


def solution(mesh):
    pair_spec = P(('batch', 'dap'), None, None)
    mask_spec = P(('batch', 'dap'), None)
    array_b8 = P(None, ('batch', 'dap'), None)

    def device_fn(pair_act, pair_mask, value_a7, opm_norm, opm_w_in, opm_b_in, opm_w_out, opm_b_out, tri_norm_in, tri_w_ab, tri_b_ab, tri_w_gate, tri_b_gate, tri_norm_out, tri_w_out, tri_b_out):
        mask_f = pair_mask.astype(jnp.float32)
        for layer_idx in range(opm_norm.shape[0]):
            value_a8, array_b9 = value_a15(value_a7, opm_norm[layer_idx], opm_w_in[layer_idx], opm_b_in[layer_idx])
            value_a14 = lax.all_gather(array_b9, 'dap', axis=1, tiled=True)
            pair_act = outer_mean_rows(pair_act, value_a8, value_a14, opm_w_out[layer_idx], opm_b_out[layer_idx])
            norm_in = tri_norm_in[layer_idx].astype(jnp.float32)
            normed = layer_norm(pair_act, norm_in[0], norm_in[1], -1)
            w_ab = tri_w_ab[layer_idx]
            b_ab = tri_b_ab[layer_idx]
            right_tri = gated_projection(normed, mask_f, w_ab[:, 2:4], b_ab[2:4])
            right_full = lax.all_gather(right_tri, 'dap', axis=1, tiled=True)
            left_tri = gated_projection(normed, mask_f, w_ab[:, 0:2], b_ab[0:2])
            tri_prod = jnp.einsum('cik,cjk->cij', left_tri, right_full, preferred_element_type=jnp.float32)
            pair_act = triangle_finish(pair_act, normed, tri_prod, tri_w_gate[layer_idx], tri_b_gate[layer_idx], tri_norm_out[layer_idx], tri_w_out[layer_idx], tri_b_out[layer_idx])
        return pair_act

    return jax.shard_map(device_fn, mesh=mesh, in_specs=(pair_spec, mask_spec, array_b8) + (P(),) * 13, out_specs=pair_spec, check_vma=False)
```

profile of v0, /device:TPU:21, one launch (start us, length us, event | category | flops | bytes accessed | tf_op | source)
XLA Modules:
  0.0 551.5 jit_solution(6898758245728842665)
XLA Ops:
  10.1 14.1 %fusion.76 = f32[512,16]{1,0:T(8,128)S(1)} fusion(bf16[512,16,256]{2,1,0:T(8,128)(2,1)S(1)} %copy-done.2, f32[512,16]{1,0:T(8,128)S(1)} %broadcast_multiply_fusion), kind=kLoop, calls=%fused_computation.48 | loop fusion | flops 8380416 | bytes 4259840 | tf_op jit(solution)/shard_map/reduce_sum | solution.py:15
  33.8 6.2 %fusion.128 = f32[512,16,32]{2,1,0:T(8,128)} fusion(bf16[512,16,256]{2,1,0:T(8,128)(2,1)} %param.22, f32[256]{0:T(256)S(1)} %bitcast.352, f32[256]{0:T(256)S(1)} %bitcast.350, f32[512,16]{1,0:T(8,128)S(1)} %add_rsqrt_fusion, f32[512,16]{1,0:T(8,128)S(1)} %broadcast_multiply_fusion, bf16[256,2,32]{0,2,1:T(8,128)(2,1)S(1)} %get-tuple-element.141), kind=kOutput, calls=%fused_computation.126 | convolution fusion | flops 146800640 | bytes 5785600 | tf_op jit(solution)/shard_map/sim,mc->sic/dot_general | solution.py:23
  44.1 6.2 %fusion.134 = f32[512,16,32]{2,1,0:T(8,128)} fusion(bf16[512,16,256]{2,1,0:T(8,128)(2,1)} %param.22, f32[256]{0:T(256)S(1)} %bitcast.355, f32[256]{0:T(256)S(1)} %bitcast.357, f32[512,16]{1,0:T(8,128)S(1)} %add_rsqrt_fusion, f32[512,16]{1,0:T(8,128)S(1)} %broadcast_multiply_fusion, bf16[256,2,32]{0,2,1:T(8,128)(2,1)S(1)} %get-tuple-element.142), kind=kOutput, calls=%fused_computation.129 | convolution fusion | flops 146800640 | bytes 5785600 | tf_op jit(solution)/shard_map/sim,mc->sic/dot_general | solution.py:22
  59.1 32.3 %all-gather.5.cloned.1.call-done = bf16[512,256,32]{0,2,1:T(8,128)(2,1)} async-done(((bf16[512,16,32]{0,2,1:T(8,128)(2,1)}), bf16[512,256,32]{0,2,1:T(8,128)(2,1)}) %all-gather.5.cloned.1.call-update) | async-done | bytes 8388624 | tf_op jit(solution)/shard_map/all_gather | solution.py:71
  91.4 44.3 %copy.40 = bf16[512,256,32]{2,1,0:T(8,128)(2,1)} copy(bf16[512,256,32]{0,2,1:T(8,128)(2,1)} %all-gather.5.cloned.1.call-done) | data formatting | bytes 16777216 | tf_op jit(solution)/shard_map/while | solution.py:45
  135.9 85.0 %while.20 = (s32[]{:T(128)}, bf16[2,8,256,128]{3,2,1,0:T(8,128)(2,1)S(1)}, bf16[2,8,256,128]{3,2,1,0:T(8,128)(2,1)}, bf16[2,512,8,32]{3,2,1,0:T(8,128)(2,1)}, bf...) while((s32[]{:T(128)}, ...), condition=%wide.region_3.4_spmd, body=%wide.region_2.3_spmd.sunk | while | flops 2690121728 | bytes 48235128 | solution.py:45
  137.2 30.7 %copy.151 = bf16[512,256,32,1]{1,0,2,3:T(8,128)(2,1)} copy(bf16[512,256,32,1]{2,1,0,3:T(8,128)(2,1)} %bitcast.341) | data formatting | bytes 16777216 | tf_op jit(solution)/shard_map
  167.8 5.0 fusion.180
  172.9 5.5 fusion.181
  179.7 30.7 %copy.151 = bf16[512,256,32,1]{1,0,2,3:T(8,128)(2,1)} copy(bf16[512,256,32,1]{2,1,0,3:T(8,128)(2,1)} %bitcast.341) | data formatting | bytes 16777216 | tf_op jit(solution)/shard_map
  210.3 5.0 fusion.180
  215.4 5.5 fusion.181
  228.4 6.2 %fusion.130 = f32[512,16,32]{2,1,0:T(8,128)} fusion(bf16[512,16,256]{2,1,0:T(8,128)(2,1)} %param.22, f32[256]{0:T(256)S(1)} %bitcast.353, f32[256]{0:T(256)S(1)} %bitcast.351, f32[512,16]{1,0:T(8,128)} %copy-done.8, f32[512,16]{1,0:T(8,128)S(1)} %copy-done.4, bf16[256,2,32]{0,2,1:T(8,128)(2,1)S(1)} %copy-done.15), kind=kOutput, calls=%fused_computation.127 | convolution fusion | flops 146800640 | bytes 5556224 | tf_op jit(solution)/shard_map/sim,mc->sic/dot_general | solution.py:22
  244.4 44.3 %copy.51 = bf16[512,256,32]{2,1,0:T(8,128)(2,1)} copy(bf16[512,256,32]{0,2,1:T(8,128)(2,1)} %all-gather.9.cloned.1.call-done) | data formatting | bytes 16777216 | tf_op jit(solution)/shard_map/while | solution.py:45
  290.1 28.9 %all-gather.7.cloned.1.call-done = bf16[128,256,256]{2,0,1:T(8,128)(2,1)} async-done(((bf16[128,16,256]{2,0,1:T(8,128)(2,1)}), bf16[128,256,256]{2,0,1:T(8,128)(2,1)}) %all-gather.7.cloned.1.call-update) | async-done | bytes 16777232 | tf_op jit(solution)/shard_map/all_gather | solution.py:78
  319.0 16.0 %fusion.156 = (f32[16,256]{1,0:T(8,128)S(1)}, f32[128,16,256]{2,1,0:T(8,128)}) fusion(bf16[128,16,256]{2,1,0:T(8,128)(2,1)S(1)} %copy.45, bf16[128,256,256]{2,0,1:T(8,128)(2,1)} %all-gather.7.cloned.1.call-done), kind=kOutput, calls=%fused_computation.208 | convolution fusion | flops 268955648 | bytes 19939328 | tf_op jit(solution)/shard_map/cik,cjk->cij/dot_general | solution.py:80
  340.5 85.2 %while.21 = (s32[]{:T(128)}, bf16[2,8,256,128]{3,2,1,0:T(8,128)(2,1)S(1)}, bf16[2,8,256,128]{3,2,1,0:T(8,128)(2,1)}, bf16[2,512,8,32]{3,2,1,0:T(8,128)(2,1)}, bf...) while((s32[]{:T(128)}, ...), condition=%wide.region_9.10_spmd, body=%wide.region_8.9_spmd.sunk | while | flops 2690121728 | bytes 48235128 | solution.py:45
  342.0 30.7 %copy.154 = bf16[512,256,32,1]{1,0,2,3:T(8,128)(2,1)} copy(bf16[512,256,32,1]{2,1,0,3:T(8,128)(2,1)} %bitcast.340) | data formatting | bytes 16777216 | tf_op jit(solution)/shard_map
  377.7 5.5 fusion.187
  384.5 30.7 %copy.154 = bf16[512,256,32,1]{1,0,2,3:T(8,128)(2,1)} copy(bf16[512,256,32,1]{2,1,0,3:T(8,128)(2,1)} %bitcast.340) | data formatting | bytes 16777216 | tf_op jit(solution)/shard_map
  415.2 5.0 fusion.186
  420.2 5.5 fusion.187
  435.2 88.2 %all-gather.11.cloned.1.call-done = bf16[128,256,256]{2,0,1:T(8,128)(2,1)} async-done(((bf16[128,16,256]{2,0,1:T(8,128)(2,1)}), bf16[128,256,256]{2,0,1:T(8,128)(2,1)}) %all-gather.11.cloned.1.call-update) | async-done | bytes 16777232 | tf_op jit(solution)/shard_map/all_gather | solution.py:78
  523.5 16.0 %fusion.157 = (f32[16,256]{1,0:T(8,128)S(1)}, f32[128,16,256]{2,1,0:T(8,128)}) fusion(bf16[128,16,256]{2,1,0:T(8,128)(2,1)S(1)} %copy.56, bf16[128,256,256]{2,0,1:T(8,128)(2,1)} %all-gather.11.cloned.1.call-done), kind=kOutput, calls=%fused_computation.209 | convolution fusion | flops 268955648 | bytes 19939328 | tf_op jit(solution)/shard_map/cik,cjk->cij/dot_general | solution.py:80
  (167 shorter events, 74.6 us)
Async XLA Ops:
  6.5 84.8 %all-gather.5.cloned.1.call-start = ((), (), s32[]{:S(2)}) async-start(), calls=%async_computation | async-start | bytes 8912896 | tf_op jit(solution)/shard_map/all_gather | solution.py:71
  6.6 3.5 copy-start.2
  10.1 34.0 %copy-start.3 = (f32[512,16]{1,0:T(8,128)}, f32[512,16]{1,0:T(8,128)S(1)}, u32[]{:S(2)}) copy-start(f32[512,16]{1,0:T(8,128)S(1)} %broadcast_multiply_fusion) | copy-start | bytes 98308
  10.1 14.2 %copy-start.19 = (bf16[2,2,256]{2,1,0:T(2,128)(2,1)S(1)}, bf16[2,2,256]{2,1,0:T(2,128)(2,1)}, u32[]{:S(2)}) copy-start(bf16[2,2,256]{2,1,0:T(2,128)(2,1)} %param.23) | copy-start | bytes 6148
  10.1 14.2 %copy-start.13 = (bf16[2,256,2,32]{1,3,2,0:T(8,128)(2,1)S(1)}, bf16[2,256,2,32]{1,3,2,0:T(8,128)(2,1)}, u32[]{:S(2)}) copy-start(bf16[2,256,2,32]{1,3,2,0:T(8,128)(2,1)} %param.24) | copy-start | bytes 196612
  24.3 19.8 %copy-start.8 = (f32[512,16]{1,0:T(8,128)}, f32[512,16]{1,0:T(8,128)S(1)}, u32[]{:S(2)}) copy-start(f32[512,16]{1,0:T(8,128)S(1)} %add_rsqrt_fusion) | copy-start | bytes 98308
  24.4 9.4 %copy-start.32 = (f32[1,1,256]{2,1,0:T(1,128)}, f32[1,1,256]{2,1,0:T(1,128)S(1)}, u32[]{:S(2)}) copy-start(f32[1,1,256]{2,1,0:T(1,128)S(1)} %get-tuple-element.159) | copy-start | bytes 3076
  24.4 9.4 %copy-start.34 = (f32[1,1,256]{2,1,0:T(1,128)}, f32[1,1,256]{2,1,0:T(1,128)S(1)}, u32[]{:S(2)}) copy-start(f32[1,1,256]{2,1,0:T(1,128)S(1)} %get-tuple-element.162) | copy-start | bytes 3076
  24.4 9.4 %copy-start.14 = (bf16[256,2,32]{0,2,1:T(8,128)(2,1)}, bf16[256,2,32]{0,2,1:T(8,128)(2,1)S(1)}, u32[]{:S(2)}) copy-start(bf16[256,2,32]{0,2,1:T(8,128)(2,1)S(1)} %get-tuple-element.141) | copy-start | bytes 98308
  33.7 210.6 %all-gather.9.cloned.1.call-start = ((), (), s32[]{:S(2)}) async-start(), calls=%async_computation.2 | async-start | bytes 8912896 | tf_op jit(solution)/shard_map/all_gather | solution.py:71
  43.8 275.2 %all-gather.7.cloned.1.call-start = ((), (), s32[]{:S(2)}) async-start(), calls=%async_computation.1 | async-start | bytes 17825792 | tf_op jit(solution)/shard_map/all_gather | solution.py:78
  53.1 3.3 copy-start.30
  53.1 3.9 copy-start.25
  53.1 4.5 copy-start.7
  53.3 5.1 copy-start.6
  55.8 169.8 %copy-start.10 = (f32[16,256]{1,0:T(8,128)}, f32[16,256]{1,0:T(8,128)S(1)}, u32[]{:S(2)}) copy-start(f32[16,256]{1,0:T(8,128)S(1)} %convert_element_type.276) | copy-start | bytes 49156
  167.8 5.0 copy-start.38
  210.3 5.0 copy-start.38
  228.3 295.2 %all-gather.11.cloned.1.call-start = ((), (), s32[]{:S(2)}) async-start(), calls=%async_computation.3 | async-start | bytes 17825792 | tf_op jit(solution)/shard_map/all_gather | solution.py:78
  237.4 4.4 copy-start.27
  237.4 4.9 copy-start.28
  237.4 5.5 copy-start.31
  372.7 5.0 copy-start.40
  415.2 5.0 copy-start.40
  (23 other events, 41.6 us)
Sparse Core Ops, SparseCore 0:
  33.8 57.5 all-gather.4
  93.0 51.0 all-gather.8
  228.4 90.5 all-gather.6
  432.9 90.5 all-gather.10
where the time goes:
time: 560 us; the launch traced here: 552 us
  local copies, waits for them, and re-layouts  242 us (43%)
  waiting for transfers between devices  150 us (27%)
  matrix products  105 us (19%)
  other arithmetic  40.1 us (7%)
  between operations  14.4 us (3%)
    another operation x6, local copies, waits for them, and re-layouts  123 us
    all_gather x2, waiting for transfers between devices, device_fn(): right_full = lax.all_gather(right_tri, 'dap', axis=1, tiled=True)  117 us
    while x2, local copies, waits for them, and re-layouts, outer_mean_rows(): lax.map(block_update, (left_blocks, pair_blocks))  88.6 us
    all_gather x2, waiting for transfers between devices, device_fn(): value_a14 = lax.all_gather(array_b9, 'dap', axis=1, tiled=True)  32.3 us
    dot_general x2, matrix products, device_fn(): jnp.einsum('cik,cjk->cij', left_tri, right_full, preferred_element_type=j...  31.9 us
    dot_general x4, matrix products, block_update(): jnp.einsum('icjd,cdz->ijz', outer_prod, w_out_r, preferred_element_type=j...  21.9 us
    reduce_sum x5, other arithmetic, layer_norm(): var_val = jnp.mean(centered * centered, axis=norm_axis, keepdims=True)  20.7 us
    dot_general x4, matrix products, block_update(): jnp.einsum('sic,sjd->icjd', left_blk, right_full, preferred_element_type=...  20.1 us
  transfers between devices with their start and end apart: 4, of which 3 were waited for; matrix products, arithmetic and copies ran while one was open for 41% of the time, Pallas kernels for 0%

commit v1 on v0

v1 whole, which is shorter than its diff:
```python
import functools

import jax
import jax.numpy as jnp
from jax import lax
from jax.experimental import pallas as pl
from jax.experimental.pallas import tpu as pltpu
from jax.sharding import PartitionSpec as P

F32 = jnp.float32
BF16 = jnp.bfloat16
EPS = 1e-5
VMEM_LIMIT = 63 * 1024 * 1024
NT = (((1,), (1,)), ((), ()))
LANES = 128

V_BQ, V_BP, V_BG, V_AP, V_AG, V_GATE, V_NI0, V_NI1, V_NO0, V_NO1, V_BO, V_BIN = range(12)


def sigmoid(x):
    return 1.0 / (1.0 + jnp.exp(-x))


def norm_rows(x, scale, offset):
    inv = 1.0 / x.shape[0]
    xc = x - jnp.sum(x, axis=0, keepdims=True) * inv
    var = jnp.sum(xc * xc, axis=0, keepdims=True) * inv
    return (xc * lax.rsqrt(var + EPS) * scale + offset).astype(BF16)


def twice(x):
    return jnp.concatenate([x, x], axis=1)


def project_kernel(m_ref, w_ref, norm_ref, bias_ref, a_ref, b_ref, scr):
    r = pl.program_id(0)
    layers, width = w_ref.shape[0], w_ref.shape[1] // 2
    seqs, dim = m_ref.shape[1], m_ref.shape[2]
    rows = b_ref.shape[1] // width
    x = m_ref[0].astype(F32)
    xc = x - jnp.sum(x, axis=1, keepdims=True) * (1.0 / dim)
    var = jnp.sum(xc * xc, axis=1, keepdims=True) * (1.0 / dim)
    xn = xc * lax.rsqrt(var + EPS)
    for l in range(layers):
        mn = (xn * norm_ref[l, 0:1] + norm_ref[l, 1:2]).astype(BF16)
        out = lax.dot_general(w_ref[l], mn, NT, preferred_element_type=F32)
        bias = bias_ref[l][: 2 * width]
        for c in range(seqs // LANES):
            part = out[:, c * LANES : (c + 1) * LANES] + bias
            a_ref[l, 0, :, c * LANES : (c + 1) * LANES] = part[:width].astype(BF16)
            scr[l, c, pl.ds(r, width, stride=rows), :] = part[width:]

    @pl.when(r == pl.num_programs(0) - 1)
    def _():
        for l in range(layers):
            for c in range(seqs // LANES):
                b_ref[l, :, c * LANES : (c + 1) * LANES] = scr[l, c].astype(BF16)


def opm_half(l, h, a_ref, b_ref, wq_ref, vec_ref, z_ref, q_ref):
    pairs, cd, lanes2 = q_ref.shape
    seqs = a_ref.shape[2]
    width = a_ref.shape[1] // (2 * pairs)
    half = lanes2 // 2
    scale = 1.0 / seqs

    def outer(t, _):
        rhs = b_ref[h, pl.ds(2 * t, 2)].reshape(2 * half, seqs)
        out = lax.dot_general(a_ref[l], rhs, NT, preferred_element_type=F32)
        out = (out * scale).astype(BF16)
        for d in range(2):
            blk = out[:, d * half : (d + 1) * half].reshape(2 * pairs, width, half)
            at = pl.ds(pl.multiple_of((2 * t + d) * width, width), width)
            for e in range(2):
                q_ref[:, at, e * half : (e + 1) * half] = blk[e * pairs : (e + 1) * pairs]
        return 0

    lax.fori_loop(0, cd // width // 2, outer, 0)
    bq = twice(vec_ref[l, V_BQ])

    def project(p, _):
        u = jnp.dot(wq_ref[l], q_ref[p], preferred_element_type=F32) + bq
        z_ref[h, p] = (z_ref[h, p].astype(F32) + u.astype(BF16).astype(F32)).astype(BF16)
        return 0

    lax.fori_loop(0, pairs, project, 0)


def gate_half(l, h, z_ref, mask_ref, wall_ref, vec_ref, fa_ref, fb_ref, g_ref, a_out, b_out):
    pairs = z_ref.shape[1]
    dim = z_ref.shape[2]
    half = z_ref.shape[3] // 2

    def project(p, _):
        zn = norm_rows(z_ref[h, p].astype(F32), twice(vec_ref[l, V_NI0]), twice(vec_ref[l, V_NI1]))
        mask = mask_ref[h, p]
        at = pl.ds(pl.multiple_of(p * dim, dim), dim)

        def proj(q, v):
            w = wall_ref[l, q * dim : (q + 1) * dim]
            return jnp.dot(w, zn, preferred_element_type=F32) + twice(vec_ref[l, v])

        for q, f_ref, vp, vg in ((0, fb_ref, V_BP, V_BG), (2, fa_ref, V_AP, V_AG)):
            val = mask * sigmoid(proj(q + 1, vg)) * proj(q, vp)
            f_ref[0, at, :] = val[:, :half]
            f_ref[1, at, :] = val[:, half:]
        g_ref[h, p] = sigmoid(proj(4, V_GATE))
        return 0

    lax.fori_loop(0, pairs, project, 0)

    def relayout(t, _):
        for u in range(8):
            c = t * 8 + u
            for f_ref, out in ((fb_ref, b_out), (fa_ref, a_out)):
                lo = f_ref[0, pl.ds(c, pairs, stride=dim), :]
                hi = f_ref[1, pl.ds(c, pairs, stride=dim), :]
                out(c, h, jnp.concatenate([lo, hi], axis=0).astype(BF16))
        return 0

    lax.fori_loop(0, dim // 8, relayout, 0)


def triangle_half(jh, a_ref, b_ref, o_ref):
    dim = a_ref.shape[0]
    pairs = a_ref.shape[1] // 2

    def step(t, _):
        for u in range(8):
            c = t * 8 + u
            o = lax.dot_general(a_ref[c], b_ref[jh, c], NT, preferred_element_type=F32)
            o_ref[0, pl.ds(c, pairs, stride=dim), :] = o[:pairs]
            o_ref[1, pl.ds(c, pairs, stride=dim), :] = o[pairs:]
        return 0

    lax.fori_loop(0, dim // 8, step, 0)


def finish_half(l, jh, o_ref, g_ref, z_ref, wo_ref, vec_ref):
    pairs = z_ref.shape[1]
    dim = z_ref.shape[2]

    def step(p, _):
        at = pl.ds(pl.multiple_of(p * dim, dim), dim)
        o = jnp.concatenate([o_ref[0, at, :], o_ref[1, at, :]], axis=1)
        on = norm_rows(o, twice(vec_ref[l, V_NO0]), twice(vec_ref[l, V_NO1]))
        u = jnp.dot(wo_ref[l], on, preferred_element_type=F32) + twice(vec_ref[l, V_BO])
        z_ref[jh, p] = (z_ref[jh, p].astype(F32) + g_ref[jh, p] * u.astype(BF16).astype(F32)).astype(BF16)
        return 0

    lax.fori_loop(0, pairs, step, 0)


def collect(src_ref, dst_ref, sem):
    devices, _, rows, _ = src_ref.shape
    copies = []
    for d in range(devices):
        dst = dst_ref.at[d % 2, :, pl.ds((d // 2) * rows, rows), :]
        copies.append(pltpu.make_async_copy(src_ref.at[d], dst, sem.at[d]))
    for copy in copies:
        copy.start()
    for copy in copies:
        copy.wait()


def head_kernel(l, b_hbm, a_ref, z_in, mask_ref, wq_ref, wall_ref, vec_ref, z_ref, at_ref, bt_ref, g_ref,
                b_buf, q_scr, fa, fb, sem):
    collect(b_hbm, b_buf, sem)
    z_ref[...] = z_in[...]

    def a_out(c, h, v):
        at_ref[c, :, h * LANES : (h + 1) * LANES] = v

    def b_out(c, h, v):
        bt_ref[c, :, h * LANES : (h + 1) * LANES] = v

    for h in range(2):
        opm_half(l, h, a_ref, b_buf, wq_ref, vec_ref, z_ref, q_scr)
        gate_half(l, h, z_ref, mask_ref, wall_ref, vec_ref, fa, fb, g_ref, a_out, b_out)


def tail_kernel(l, bt_hbm, at_ref, g_ref, z_in, wo_ref, vec_ref, z_ref, b_buf, o_scr, sem):
    collect(bt_hbm, b_buf, sem)
    z_ref[...] = z_in[...]
    for jh in range(2):
        triangle_half(jh, at_ref, b_buf, o_scr)
        finish_half(l, jh, o_scr, g_ref, z_ref, wo_ref, vec_ref)


def solution(mesh):
    size = mesh.shape["dap"]
    chips = size // 2
    pair_spec = P(("batch", "dap"), None, None)
    mask_spec = P(("batch", "dap"), None)
    msa_spec = P(None, ("batch", "dap"), None)
    any_spec = pl.BlockSpec(memory_space=pl.ANY)
    vmem_spec = pl.BlockSpec(memory_space=pltpu.VMEM)

    def device_fn(pair_act, pair_mask, msa_act, opm_norm, opm_w_in, opm_b_in, opm_w_out, opm_b_out, tri_norm_in,
                  tri_w_ab, tri_b_ab, tri_w_gate, tri_b_gate, tri_norm_out, tri_w_out, tri_b_out):
        rows, cols, dim = pair_act.shape
        seqs, _, mdim = msa_act.shape
        layers = opm_norm.shape[0]
        width = opm_w_in.shape[-1]
        pairs = rows // 2
        half = cols // 2

        w_in = jnp.transpose(opm_w_in, (0, 2, 3, 1)).reshape(layers, 2 * width, mdim)
        wq = jnp.transpose(opm_w_out.reshape(layers, width, width, dim), (0, 3, 2, 1)).reshape(layers, dim, -1)
        w5 = jnp.concatenate([tri_w_ab[:, :, 2:4], tri_w_ab[:, :, 0:2], tri_w_gate[:, :, None]], axis=2)
        wall = jnp.transpose(w5, (0, 2, 3, 1)).reshape(layers, 5 * dim, dim)
        wo = jnp.transpose(tri_w_out, (0, 2, 1))
        b_in = jnp.pad(opm_b_in.reshape(layers, 1, 2 * width), ((0, 0), (0, 0), (0, dim - 2 * width)))
        vec = jnp.concatenate([opm_b_out[:, None], tri_b_ab[:, 2:4], tri_b_ab[:, 0:2], tri_b_gate[:, None],
                               tri_norm_in, tri_norm_out, tri_b_out[:, None], b_in], axis=1).astype(F32)
        vec = jnp.broadcast_to(vec[..., None], vec.shape + (LANES,))

        z = pair_act.reshape(2, pairs, chips, 2, rows, dim)
        z = jnp.transpose(z, (3, 1, 5, 0, 2, 4)).reshape(2, pairs, dim, 2 * half)
        mask = pair_mask.astype(F32).reshape(2, pairs, chips, 2, rows)
        mask = jnp.transpose(mask, (3, 1, 0, 2, 4)).reshape(2, pairs, 1, 2 * half)
        m = jnp.swapaxes(msa_act, 0, 1)

        a, b = pl.pallas_call(
            project_kernel,
            grid=(rows,),
            out_shape=(jax.ShapeDtypeStruct((layers, rows, width, seqs), BF16),
                       jax.ShapeDtypeStruct((layers, width * rows, seqs), BF16)),
            in_specs=[pl.BlockSpec((1, seqs, mdim), lambda r: (r, 0, 0)),
                      pl.BlockSpec(w_in.shape, lambda r: (0, 0, 0)),
                      pl.BlockSpec(opm_norm.shape, lambda r: (0, 0, 0)),
                      pl.BlockSpec((layers, dim, LANES), lambda r: (0, 0, 0))],
            out_specs=(pl.BlockSpec((layers, 1, width, seqs), lambda r: (0, r, 0, 0)),
                       pl.BlockSpec((layers, width * rows, seqs), lambda r: (0, 0, 0))),
            scratch_shapes=[pltpu.VMEM((layers, seqs // LANES, width * rows, LANES), F32)],
            compiler_params=pltpu.CompilerParams(vmem_limit_bytes=VMEM_LIMIT),
            name="project",
        )(m, w_in, opm_norm.astype(F32), vec[:, V_BIN])
        a = a.reshape(layers, rows * width, seqs)
        b = b.reshape(layers, width, rows, seqs)

        z_shape = jax.ShapeDtypeStruct((2, pairs, dim, 2 * half), BF16)
        t_shape = jax.ShapeDtypeStruct((dim, rows, cols), BF16)
        g_shape = jax.ShapeDtypeStruct((2, pairs, dim, 2 * half), F32)
        gathered = [lax.all_gather(b[l], "dap") for l in range(layers)]
        for l in range(layers):
            z, at, bt, g = pl.pallas_call(
                functools.partial(head_kernel, l),
                out_shape=(z_shape, t_shape, t_shape, g_shape),
                in_specs=[any_spec] + [vmem_spec] * 6,
                out_specs=(vmem_spec,) * 4,
                scratch_shapes=[pltpu.VMEM((2, width, half, seqs), BF16),
                                pltpu.VMEM((pairs, width * width, 2 * half), BF16),
                                pltpu.VMEM((2, pairs * dim, LANES), F32),
                                pltpu.VMEM((2, pairs * dim, LANES), F32),
                                pltpu.SemaphoreType.DMA((size,))],
                compiler_params=pltpu.CompilerParams(vmem_limit_bytes=VMEM_LIMIT),
                name="head",
            )(gathered[l], a, z, mask, wq, wall, vec)
            bt = lax.all_gather(bt, "dap")
            z = pl.pallas_call(
                functools.partial(tail_kernel, l),
                out_shape=z_shape,
                in_specs=[any_spec] + [vmem_spec] * 5,
                out_specs=vmem_spec,
                scratch_shapes=[pltpu.VMEM((2, dim, half, cols), BF16),
                                pltpu.VMEM((2, pairs * dim, LANES), F32),
                                pltpu.SemaphoreType.DMA((size,))],
                compiler_params=pltpu.CompilerParams(vmem_limit_bytes=VMEM_LIMIT),
                name="tail",
            )(bt, at, g, z, wo, vec)
        out = z.reshape(2, pairs, dim, 2, chips, rows)
        return jnp.transpose(out, (3, 1, 4, 0, 5, 2)).reshape(rows, cols, dim)

    return jax.shard_map(device_fn, mesh=mesh, in_specs=(pair_spec, mask_spec, msa_spec) + (P(),) * 13,
                         out_specs=pair_spec, check_vma=False)
```

time: 560 us -> 423 us (0.76); the launches traced: 552 us -> 422 us
  local copies, waits for them, and re-layouts: 242 us -> 23.9 us
  Pallas kernels: 0 us -> 120 us
  waiting for transfers between devices: 150 us -> 264 us
  matrix products: 105 us -> 0 us
  other arithmetic: 40.1 us -> 1.04 us
    another operation x6 -> x0, local copies, waits for them, and re-layouts: 123 us -> none
    pallas_call x0 -> x5, Pallas kernels: none -> 120 us  [the longest x2 62.9 us: device_fn(): pl.pallas_call(functools.partial(head_kernel, l), out_shape=(z_shape, t_s...]
    all_gather x4, waiting for transfers between devices: 149 us -> 263 us  [the longest x2 180 us: device_fn(): bt = lax.all_gather(bt, 'dap')]
    dot_general x22 -> x0, matrix products: 105 us -> none  [the longest x2 31.9 us: device_fn(): jnp.einsum('cik,cjk->cij', left_tri, right_full, preferred_element_type=j...]
    while x10 -> x0, local copies, waits for them, and re-layouts: 88.6 us -> none  [the longest x2 88.6 us: outer_mean_rows(): lax.map(block_update, (left_blocks, pair_blocks))]
    reduce_sum x8 -> x0, other arithmetic: 24.9 us -> none  [the longest x5 20.7 us: layer_norm(): var_val = jnp.mean(centered * centered, axis=norm_axis, keepdims=True)]
    convert_element_type x20 -> x2, other arithmetic: 15 us -> 0.59 us  [the longest x1 0.59 us: device_fn(): opm_norm.astype(F32)]
    dot_general x4 -> x0, local copies, waits for them, and re-layouts: 11.2 us -> none  [the longest x2 5.61 us: value_a15(): jnp.einsum('sim,mc->sic', normed, w_in[:, 1, :], preferred_element_type=j...]
  transfers between devices with their start and end apart: 4 -> 4, of which waited for: 3 -> 4; matrix products, arithmetic and copies ran while one was open for 41% -> 1% of each run, Pallas kernels for 0% -> 5%
where the time goes in v1:
time: 423 us; the launch traced here: 422 us
  waiting for transfers between devices  264 us (62%)
  Pallas kernels  120 us (28%)
  local copies, waits for them, and re-layouts  23.9 us (6%)
  between operations  13.3 us (3%)
    all_gather x2, waiting for transfers between devices, device_fn(): bt = lax.all_gather(bt, 'dap')  180 us
    all_gather x2, waiting for transfers between devices, device_fn(): gathered = [lax.all_gather(b[l], 'dap') for l in range(layers)]  83 us
    pallas_call x2, Pallas kernels, device_fn(): pl.pallas_call(functools.partial(head_kernel, l), out_shape=(z_shape, t_s...  62.9 us
    pallas_call x2, Pallas kernels, device_fn(): pl.pallas_call(functools.partial(tail_kernel, l), out_shape=z_shape, in_s...  43.2 us
    pallas_call x1, Pallas kernels, device_fn(): pl.pallas_call(project_kernel, grid=(rows,), out_shape=(jax.ShapeDtypeStr...  13.9 us
  transfers between devices with their start and end apart: 4, of which 4 were waited for; matrix products, arithmetic and copies ran while one was open for 1% of the time, Pallas kernels for 5%

profile of v1, /device:TPU:21, one launch (start us, length us, event | category | flops | bytes accessed | tf_op | source)
XLA Modules:
  0.0 422.1 jit_solution(18202543240176350363)
XLA Ops:
  6.6 0.8 fusion.2
  7.3 0.8 reshape.114
  10.1 1.4 concatenate.19
  11.5 5.6 %copy.75 = bf16[512,16,256]{2,0,1:T(8,128)(2,1)} copy(bf16[512,16,256]{2,1,0:T(8,128)(2,1)} %param.18) | data formatting | bytes 8388608 | tf_op args[2]
  17.7 0.8 broadcast_in_dim.17.bias_ref
  18.4 13.9 %project.1 = (bf16[2,16,32,512]{3,2,1,0:T(8,128)(2,1)}, bf16[2,512,512]{2,1,0:T(8,128)(2,1)}) custom-call(bf16[16,512,256]{2,1,0:T(8,128)(2,1)} %bitcast.39, bf16[2,64,256]{2,1,0:T(8,128)(2,1)} %bitcast.54, f32[2,2,256]{2,1,0:T(2,128)} %convert_element_type.15.norm_ref, f32[2,128,128]{2,1,0:T(8,128)} %broadcast_in_dim.17.bias_ref), custom_call_target="tpu_custom_call" | custom-call | tf_op jit(solution)/shard_map/project/pallas_call | solution.py:224
  32.3 2.4 fusion
  35.6 1.0 copy.65
  36.8 1.0 copy.67.wq_ref
  38.1 0.7 reshape.106.mask_ref
  39.1 1.3 copy.66.z_in
  40.4 52.0 %all-gather.9.cloned.1.call-done.b_hbm = bf16[16,32,16,512]{3,2,1,0:T(8,128)(2,1)} async-done(((bf16[1,32,16,512]{3,2,1,0:T(8,128)(2,1)}), bf16[16,32,16,512]{3,2,1,0:T(8,128)(2,1)}) %all-gather.9.cloned.1.call-update) | async-done | bytes 8388624 | tf_op jit(solution)/shard_map/all_gather | solution.py:245
  92.4 1.6 broadcast_in_dim.19.vec_ref
  94.0 31.4 %head.2 = (bf16[2,8,128,256]{3,2,1,0:T(8,128)(2,1)}, bf16[128,16,256]{2,1,0:T(8,128)(2,1)}, bf16[128,16,256]{2,1,0:T(8,128)(2,1)}, f32[2,8,128,256]{3,2,1,0:T(8,128)}) custom-call(bf16[16,32,16,512]{3,2,1,0:T(8,128)(2,1)} %all-gather.9.cloned.1.call-done.b_hbm, bf16[2,512,512]{2,1,0:T(8,128)(2,1)} %bitcast.40, bf16[2,8,128,256]{3,2,1,0:T(8,128)(2,1)} %copy.66.z_in, ...), custom_call_target="tpu_custom_call" | custom-call | tf_op jit(solution)/shard_map/head/pallas_call | solution.py:247
  125.6 0.7 all-gather.7.cloned.1.call-update
  126.4 0.7 copy.68
  127.1 89.1 %all-gather.11.cloned.1.call-done = bf16[2048,16,256]{2,1,0:T(8,128)(2,1)} async-done(((bf16[128,16,256]{2,1,0:T(8,128)(2,1)}), bf16[2048,16,256]{2,1,0:T(8,128)(2,1)}) %all-gather.11.cloned.1.call-update) | async-done | bytes 16777232 | tf_op jit(solution)/shard_map/all_gather | solution.py:260
  216.2 21.6 %tail.2.z_in = bf16[2,8,128,256]{3,2,1,0:T(8,128)(2,1)} custom-call(bf16[16,128,16,256]{3,2,1,0:T(8,128)(2,1)} %bitcast.37, bf16[128,16,256]{2,1,0:T(8,128)(2,1)} %get-tuple-element.18.at_ref, f32[2,8,128,256]{3,2,1,0:T(8,128)} %get-tuple-element.19.g_ref, bf16[2,8,128,256]{3,2,1,0:T(8,128)(2,1)} %get-tuple-element.20.z_in, bf16[2,128,128]{2,1,0:T(8,128)(2,1)} %bitcast.50, ...), custom_call_target="tpu_custom_call" | custom-call | tf_op jit(solution)/shard_map/tail/pallas_call | solution.py:261
  237.9 31.1 %all-gather.7.cloned.1.call-done.b_hbm = bf16[16,32,16,512]{3,2,1,0:T(8,128)(2,1)} async-done(((bf16[1,32,16,512]{3,2,1,0:T(8,128)(2,1)}), bf16[16,32,16,512]{3,2,1,0:T(8,128)(2,1)}) %all-gather.7.cloned.1.call-update) | async-done | bytes 8388624 | tf_op jit(solution)/shard_map/all_gather | solution.py:245
  268.9 31.4 %head.3 = (bf16[2,8,128,256]{3,2,1,0:T(8,128)(2,1)}, bf16[128,16,256]{2,1,0:T(8,128)(2,1)}, bf16[128,16,256]{2,1,0:T(8,128)(2,1)}, f32[2,8,128,256]{3,2,1,0:T(8,128)}) custom-call(bf16[16,32,16,512]{3,2,1,0:T(8,128)(2,1)} %all-gather.7.cloned.1.call-done.b_hbm, bf16[2,512,512]{2,1,0:T(8,128)(2,1)} %bitcast.41, bf16[2,8,128,256]{3,2,1,0:T(8,128)(2,1)} %tail.2.z_in, ...), custom_call_target="tpu_custom_call" | custom-call | tf_op jit(solution)/shard_map/head/pallas_call | solution.py:247
  300.4 90.7 %all-gather.13.cloned.1.call-done = bf16[2048,16,256]{2,1,0:T(8,128)(2,1)} async-done(((bf16[128,16,256]{2,1,0:T(8,128)(2,1)}), bf16[2048,16,256]{2,1,0:T(8,128)(2,1)}) %all-gather.13.cloned.1.call-update) | async-done | bytes 16777232 | tf_op jit(solution)/shard_map/all_gather | solution.py:260
  391.2 21.6 %tail.3 = bf16[2,8,128,256]{3,2,1,0:T(8,128)(2,1)} custom-call(bf16[16,128,16,256]{3,2,1,0:T(8,128)(2,1)} %bitcast.38, bf16[128,16,256]{2,1,0:T(8,128)(2,1)} %get-tuple-element.22.at_ref, f32[2,8,128,256]{3,2,1,0:T(8,128)} %get-tuple-element.23.g_ref, bf16[2,8,128,256]{3,2,1,0:T(8,128)(2,1)} %get-tuple-element.24.z_in, bf16[2,128,128]{2,1,0:T(8,128)(2,1)} %bitcast.51, ...), custom_call_target="tpu_custom_call" | custom-call | tf_op jit(solution)/shard_map/tail/pallas_call | solution.py:261
  412.7 1.6 copy.70
  414.4 1.2 copy.71
  (35 shorter events, 4.4 us)
Async XLA Ops:
  6.5 85.9 %all-gather.9.cloned.1.call-start = ((), (), s32[]{:S(2)}) async-start(), calls=%async_computation.1 | async-start | bytes 8912896 | tf_op jit(solution)/shard_map/all_gather | solution.py:245
  11.5 5.6 %copy-start.6 = (bf16[2,2,256]{2,1,0:T(2,128)(2,1)S(1)}, bf16[2,2,256]{2,1,0:T(2,128)(2,1)}, u32[]{:S(2)}) copy-start(bf16[2,2,256]{2,1,0:T(2,128)(2,1)} %param.19) | copy-start | bytes 6148
  17.1 17.7 %copy-start.3 = (bf16[2,128,128]{2,1,0:T(8,128)(2,1)S(1)}, bf16[2,128,128]{2,1,0:T(8,128)(2,1)}, u32[]{:S(2)}) copy-start(bf16[2,128,128]{2,1,0:T(8,128)(2,1)} %param.27) | copy-start | bytes 196612
  17.1 17.8 %copy-start.2 = (bf16[2,128,4,128]{3,2,1,0:T(4,128)(2,1)S(1)}, bf16[2,128,4,128]{3,2,1,0:T(4,128)(2,1)}, u32[]{:S(2)}) copy-start(bf16[2,128,4,128]{3,2,1,0:T(4,128)(2,1)} %param.25) | copy-start | bytes 786436
  18.4 18.1 %copy-start.1 = (bf16[2,1024,128]{2,1,0:T(8,128)(2,1)S(1)}, bf16[2,1024,128]{2,1,0:T(8,128)(2,1)}, u32[]{:S(2)}) copy-start(bf16[2,1024,128]{2,1,0:T(8,128)(2,1)} %param.22) | copy-start | bytes 1572868
  32.3 5.5 %copy-start.5 = (s32[16,256]{1,0:T(8,128)S(1)}, s32[16,256]{1,0:T(8,128)}, u32[]{:S(2)}) copy-start(s32[16,256]{1,0:T(8,128)} %param.17) | copy-start | bytes 49156
  32.3 6.5 %copy-start = (bf16[16,256,128]{2,1,0:T(8,128)(2,1)S(1)}, bf16[16,256,128]{2,1,0:T(8,128)(2,1)}, u32[]{:S(2)}) copy-start(bf16[16,256,128]{2,1,0:T(8,128)(2,1)} %param.16) | copy-start | bytes 3145732
  34.7 181.5 %all-gather.11.cloned.1.call-start = ((), (), s32[]{:S(2)}) async-start(), calls=%async_computation.2 | async-start | bytes 17825792 | tf_op jit(solution)/shard_map/all_gather | solution.py:260
  94.0 32.4 %copy-start.4 = (bf16[2,128,128]{2,1,0:T(8,128)(2,1)S(1)}, bf16[2,128,128]{2,1,0:T(8,128)(2,1)}, u32[]{:S(2)}) copy-start(bf16[2,128,128]{2,1,0:T(8,128)(2,1)} %param.30) | copy-start | bytes 196612
  125.5 143.4 %all-gather.7.cloned.1.call-start = ((), (), s32[]{:S(2)}) async-start(), calls=%async_computation | async-start | bytes 8912896 | tf_op jit(solution)/shard_map/all_gather | solution.py:245
  126.3 264.8 %all-gather.13.cloned.1.call-start = ((), (), s32[]{:S(2)}) async-start(), calls=%async_computation.3 | async-start | bytes 17825792 | tf_op jit(solution)/shard_map/all_gather | solution.py:260
Sparse Core Ops, SparseCore 0:
  34.9 57.5 all-gather.8
  125.6 90.5 all-gather.10
  217.9 51.0 all-gather.6
  300.6 90.5 all-gather.12

commit v2 on v1

--- a/solution.py
+++ b/solution.py
@@ -109,16 +109,16 @@
 
     lax.fori_loop(0, pairs, project, 0)
 
-    def relayout(t, _):
-        for u in range(8):
-            c = t * 8 + u
-            for f_ref, out in ((fb_ref, b_out), (fa_ref, a_out)):
+    for f_ref, out in ((fb_ref, b_out), (fa_ref, a_out)):
+        def relayout(t, _):
+            for u in range(8):
+                c = t * 8 + u
                 lo = f_ref[0, pl.ds(c, pairs, stride=dim), :]
                 hi = f_ref[1, pl.ds(c, pairs, stride=dim), :]
                 out(c, h, jnp.concatenate([lo, hi], axis=0).astype(BF16))
-        return 0
-
-    lax.fori_loop(0, dim // 8, relayout, 0)
+            return 0
+
+        lax.fori_loop(0, dim // 8, relayout, 0)
 
 
 def triangle_half(jh, a_ref, b_ref, o_ref):
@@ -151,40 +151,223 @@
     lax.fori_loop(0, pairs, step, 0)
 
 
-def collect(src_ref, dst_ref, sem):
-    devices, _, rows, _ = src_ref.shape
-    copies = []
-    for d in range(devices):
-        dst = dst_ref.at[d % 2, :, pl.ds((d // 2) * rows, rows), :]
-        copies.append(pltpu.make_async_copy(src_ref.at[d], dst, sem.at[d]))
-    for copy in copies:
-        copy.start()
-    for copy in copies:
-        copy.wait()
-
-
-def head_kernel(l, b_hbm, a_ref, z_in, mask_ref, wq_ref, wall_ref, vec_ref, z_ref, at_ref, bt_ref, g_ref,
-                b_buf, q_scr, fa, fb, sem):
-    collect(b_hbm, b_buf, sem)
-    z_ref[...] = z_in[...]
-
-    def a_out(c, h, v):
-        at_ref[c, :, h * LANES : (h + 1) * LANES] = v
-
-    def b_out(c, h, v):
-        bt_ref[c, :, h * LANES : (h + 1) * LANES] = v
-
-    for h in range(2):
-        opm_half(l, h, a_ref, b_buf, wq_ref, vec_ref, z_ref, q_scr)
+class Stream:
+    def __init__(self, buf, color, lo, lanes, rows, sems, where):
+        self.buf, self.color, self.rows, self.lanes = buf, color, rows, lanes
+        self.base, self.size = lo
+        self.part = buf.shape[0] // 2
+        self.ring_send, self.ring_recv, self.core_send, self.core_recv = sems
+        self.chip, self.core, self.chips = where
+        self.sent = []
+
+    def block(self, chip, part, piece=None):
+        lo, n = part * self.part + self.base, self.size
+        if piece is not None:
+            n = n // 2
+            lo = lo + piece * n
+        rows = pl.ds(pl.multiple_of(chip * self.rows, self.rows), self.rows)
+        return self.buf.at[pl.ds(lo, n), rows, self.lanes]
+
+    def copy(self, ref, send, recv, chip, core):
+        return pltpu.make_async_remote_copy(
+            src_ref=ref, dst_ref=ref, send_sem=send, recv_sem=recv,
+            device_id={"dap": chip * 2 + core}, device_id_type=pl.DeviceIdType.MESH)
+
+    def near(self, step):
+        return lax.rem(self.chip + step + self.chips, self.chips)
+
+    def ring(self, side, hop, chip, piece=None):
+        return self.copy(self.block(chip, self.core, piece), self.ring_send.at[side, hop], self.ring_recv.at[side, hop],
+                         self.near(1 - 2 * side), self.core)
+
+    def across(self, slot, chip, part, piece=None):
+        return self.copy(self.block(chip, part, piece), self.core_send.at[slot], self.core_recv.at[slot],
+                         self.chip, 1 - self.core)
+
+    def event(self, hop):
+        if hop == 0:
+            @pl.when(self.core == self.color)
+            def _():
+                self.across(0, self.chip, 1 - self.core).start()
+                for side in range(2):
+                    self.ring(side, 0, self.chip).start()
+                self.across(1, self.chip, self.core).start()
+
+            @pl.when(self.core != self.color)
+            def _():
+                self.across(0, self.chip, self.core).wait_recv()
+                for side in range(2):
+                    self.ring(side, 0, self.chip).start()
+            return
+        last = self.chips // 2
+        for side in range(2):
+            origin = self.near((2 * side - 1) * hop)
+            piece = side if hop == last else None
+            self.ring(side, hop - 1, origin, piece).wait_recv()
+            if hop < last:
+                self.ring(side, hop, origin, side if hop == last - 1 else None).start()
+            self.across(2 + 2 * (hop - 1) + side, origin, self.core, piece).start()
+
+    def finish(self):
+        last = self.chips // 2
+
+        @pl.when(self.core != self.color)
+        def _():
+            self.across(1, self.chip, 1 - self.core).wait_recv()
+
+        for hop in range(1, last + 1):
+            for side in range(2):
+                origin = self.near((2 * side - 1) * hop)
+                piece = side if hop == last else None
+                self.across(2 + 2 * (hop - 1) + side, origin, 1 - self.core, piece).wait_recv()
+
+    def drain(self):
+        last = self.chips // 2
+
+        @pl.when(self.core == self.color)
+        def _():
+            self.across(0, self.chip, 1 - self.core).wait_send()
+            self.across(1, self.chip, self.core).wait_send()
+
+        for side in range(2):
+            for hop in range(last):
+                self.ring(side, hop, self.chip, side if hop == last - 1 else None).wait_send()
+            for hop in range(1, last + 1):
+                self.across(2 + 2 * (hop - 1) + side, self.chip, self.core, side if hop == last else None).wait_send()
+
+
+N_STREAMS = 12
+
+
+def step_kernel(chips, a_hbm, b_hbm, z_hbm, mask_ref, wq_ref, wall_ref, wo_ref, vec_ref, out_hbm,
+                b_buf, t_buf, a_ref, z_ref, at_ref, g_ref, q_scr, fa, fb,
+                ring_send, ring_recv, core_send, core_recv, local_sem):
+    me = lax.axis_index("dap")
+    chip, core = me // 2, lax.rem(me, 2)
+    rows = b_hbm.shape[2]
+    own = pl.ds(pl.multiple_of(chip * rows, rows), rows)
+    layers = b_hbm.shape[0]
+    dim = at_ref.shape[1]
+    half = z_ref.shape[3] // 2
+
+    barrier = pltpu.get_barrier_semaphore()
+    right, left = lax.rem(chip + 1, chips), lax.rem(chip + chips - 1, chips)
+    for there in (right * 2 + core, left * 2 + core, chip * 2 + 1 - core):
+        pl.semaphore_signal(barrier, inc=1, device_id={"dap": there}, device_id_type=pl.DeviceIdType.MESH)
+
+    loads = [pltpu.make_async_copy(b_hbm.at[l], b_buf.at[l, core, :, own, :], local_sem.at[l]) for l in range(layers)]
+    loads.append(pltpu.make_async_copy(a_hbm, a_ref, local_sem.at[2]))
+    loads.append(pltpu.make_async_copy(z_hbm, z_ref, local_sem.at[3]))
+    for load in loads:
+        load.start()
+    pl.semaphore_wait(barrier, 3)
+
+    where = (chip, core, chips)
+
+    def stream(n, buf, color, lo, lanes):
+        sems = tuple(s.at[n] for s in (ring_send, ring_recv, core_send, core_recv))
+        return Stream(buf, color, lo, lanes, rows, sems, where)
+
+    width = b_buf.shape[2]
+    full_b = pl.ds(0, b_buf.shape[4])
+    full_t = pl.ds(0, 2 * half)
+    b1 = [stream(q, b_buf.at[0, q], q, (0, width // 2), full_b) for q in range(2)]
+    b2 = [stream(2 + q, b_buf.at[1, q], q, (0, width // 2), full_b) for q in range(2)]
+    t1 = [[stream(4 + 2 * q + s, t_buf.at[0, q], q, (s * dim // 4, dim // 4), full_t) for s in range(2)]
+          for q in range(2)]
+    t2 = [[stream(8 + 2 * k + q, t_buf.at[1, q], q, (0, dim // 2), pl.ds(k * half, half)) for q in range(2)]
+          for k in range(2)]
+
+    def opm(l, h):
+        opm_half(l, h, a_ref, b_buf.at[l], wq_ref, vec_ref, z_ref, q_scr)
+
+    def gate(l, h):
+        def a_out(c, h, v):
+            at_ref[l, c, :, h * LANES : (h + 1) * LANES] = v
+
+        def b_out(c, h, v):
+            t_buf[l, core, c, own, h * LANES : (h + 1) * LANES] = v
+
         gate_half(l, h, z_ref, mask_ref, wall_ref, vec_ref, fa, fb, g_ref, a_out, b_out)
 
-
-def tail_kernel(l, bt_hbm, at_ref, g_ref, z_in, wo_ref, vec_ref, z_ref, b_buf, o_scr, sem):
-    collect(bt_hbm, b_buf, sem)
-    z_ref[...] = z_in[...]
-    for jh in range(2):
-        triangle_half(jh, at_ref, b_buf, o_scr)
-        finish_half(l, jh, o_scr, g_ref, z_ref, wo_ref, vec_ref)
+    def triangle(l, jh):
+        triangle_half(jh, at_ref.at[l], t_buf.at[l], fa)
+
+    def finish(l, jh):
+        finish_half(l, jh, fa, g_ref, z_ref, wo_ref, vec_ref)
+
+    def events(hop, *streams):
+        for s in streams:
+            s.event(hop)
+
+    loads[0].wait()
+    events(0, *b1)
+    loads[1].wait()
+    events(1, *b1)
+    events(2, *b1)
+    loads[2].wait()
+    loads[3].wait()
+    events(3, *b1)
+    events(0, *b2)
+    events(4, *b1)
+    b1[0].finish()
+    opm(0, 0)
+    events(1, b2[0])
+    b1[1].finish()
+    opm(0, 1)
+    events(1, b2[1])
+    gate(0, 0)
+    events(2, b2[0])
+    gate(0, 1)
+    events(2, b2[1])
+    events(0, *t1[0])
+    events(3, *b2)
+    events(1, *t1[0])
+    events(4, *b2)
+    events(2, *t1[0])
+    events(0, *t1[1])
+    events(3, *t1[0])
+    events(4, *t1[0])
+    for s in t1[0]:
+        s.finish()
+    triangle(0, 0)
+    events(1, *t1[1])
+    finish(0, 0)
+    events(2, t1[1][0])
+    for s in b2:
+        s.finish()
+    opm(1, 0)
+    events(2, t1[1][1])
+    events(3, *t1[1])
+    gate(1, 0)
+    events(0, *t2[0])
+    events(4, *t1[1])
+    for s in t1[1]:
+        s.finish()
+    triangle(0, 1)
+    finish(0, 1)
+    events(1, *t2[0])
+    opm(1, 1)
+    events(2, *t2[0])
+    gate(1, 1)
+    events(0, *t2[1])
+    events(3, *t2[0])
+    events(1, *t2[1])
+    events(4, *t2[0])
+    events(2, *t2[1])
+    events(3, *t2[1])
+    events(4, *t2[1])
+    for q in range(2):
+        t2[0][q].finish()
+        t2[1][q].finish()
+        triangle(1, q)
+        finish(1, q)
+        store = pltpu.make_async_copy(z_ref.at[q], out_hbm.at[q], local_sem.at[q])
+        store.start()
+    for s in b1 + b2 + t1[0] + t1[1] + t2[0] + t2[1]:
+        s.drain()
+    for q in range(2):
+        pltpu.make_async_copy(z_ref.at[q], out_hbm.at[q], local_sem.at[q]).wait()
 
 
 def solution(mesh):
@@ -239,36 +422,29 @@
         a = a.reshape(layers, rows * width, seqs)
         b = b.reshape(layers, width, rows, seqs)
 
-        z_shape = jax.ShapeDtypeStruct((2, pairs, dim, 2 * half), BF16)
-        t_shape = jax.ShapeDtypeStruct((dim, rows, cols), BF16)
-        g_shape = jax.ShapeDtypeStruct((2, pairs, dim, 2 * half), F32)
-        gathered = [lax.all_gather(b[l], "dap") for l in range(layers)]
-        for l in range(layers):
-            z, at, bt, g = pl.pallas_call(
-                functools.partial(head_kernel, l),
-                out_shape=(z_shape, t_shape, t_shape, g_shape),
-                in_specs=[any_spec] + [vmem_spec] * 6,
-                out_specs=(vmem_spec,) * 4,
-                scratch_shapes=[pltpu.VMEM((2, width, half, seqs), BF16),
-                                pltpu.VMEM((pairs, width * width, 2 * half), BF16),
-                                pltpu.VMEM((2, pairs * dim, LANES), F32),
-                                pltpu.VMEM((2, pairs * dim, LANES), F32),
-                                pltpu.SemaphoreType.DMA((size,))],
-                compiler_params=pltpu.CompilerParams(vmem_limit_bytes=VMEM_LIMIT),
-                name="head",
-            )(gathered[l], a, z, mask, wq, wall, vec)
-            bt = lax.all_gather(bt, "dap")
-            z = pl.pallas_call(
-                functools.partial(tail_kernel, l),
-                out_shape=z_shape,
-                in_specs=[any_spec] + [vmem_spec] * 5,
-                out_specs=vmem_spec,
-                scratch_shapes=[pltpu.VMEM((2, dim, half, cols), BF16),
-                                pltpu.VMEM((2, pairs * dim, LANES), F32),
-                                pltpu.SemaphoreType.DMA((size,))],
-                compiler_params=pltpu.CompilerParams(vmem_limit_bytes=VMEM_LIMIT),
-                name="tail",
-            )(bt, at, g, z, wo, vec)
+        hops = chips // 2
+        z = pl.pallas_call(
+            functools.partial(step_kernel, chips),
+            out_shape=jax.ShapeDtypeStruct(z.shape, BF16),
+            in_specs=[any_spec] * 3 + [vmem_spec] * 5,
+            out_specs=any_spec,
+            scratch_shapes=[pltpu.VMEM((layers, 2, width, half, seqs), BF16),
+                            pltpu.VMEM((layers, 2, dim, half, cols), BF16),
+                            pltpu.VMEM(a.shape, BF16),
+                            pltpu.VMEM(z.shape, BF16),
+                            pltpu.VMEM((layers, dim, rows, cols), BF16),
+                            pltpu.VMEM(z.shape, F32),
+                            pltpu.VMEM((pairs, width * width, 2 * half), BF16),
+                            pltpu.VMEM((2, pairs * dim, LANES), F32),
+                            pltpu.VMEM((2, pairs * dim, LANES), F32),
+                            pltpu.SemaphoreType.DMA((N_STREAMS, 2, hops)),
+                            pltpu.SemaphoreType.DMA((N_STREAMS, 2, hops)),
+                            pltpu.SemaphoreType.DMA((N_STREAMS, 2 + 2 * hops)),
+                            pltpu.SemaphoreType.DMA((N_STREAMS, 2 + 2 * hops)),
+                            pltpu.SemaphoreType.DMA((4,))],
+            compiler_params=pltpu.CompilerParams(vmem_limit_bytes=VMEM_LIMIT, collective_id=0, has_side_effects=True),
+            name="layers",
+        )(a, b, z, mask, wq, wall, wo, vec)
         out = z.reshape(2, pairs, dim, 2, chips, rows)
         return jnp.transpose(out, (3, 1, 4, 0, 5, 2)).reshape(rows, cols, dim)
 

time: 423 us -> 313 us (0.74)
  waiting for transfers between devices: 264 us -> 0 us
  Pallas kernels: 120 us -> 290 us
  between operations: 13.3 us -> 0.11 us
    all_gather x4 -> x0, waiting for transfers between devices: 263 us -> none  [the longest x2 180 us: device_fn(): bt = lax.all_gather(bt, 'dap')]
    pallas_call x4 -> x1, Pallas kernels: 106 us -> 276 us  [device_fn(): pl.pallas_call(functools.partial(step_kernel, chips), out_shape=jax.Shape...]
  transfers between devices with their start and end apart: 4 -> 0, of which waited for: 4 -> 0; matrix products, arithmetic and copies ran while one was open for 1% -> 0% of each run, Pallas kernels for 5% -> 0%
where the time goes in v2:
time: 313 us
  Pallas kernels  290 us (93%)
  local copies, waits for them, and re-layouts  21.5 us (7%)
    pallas_call x1, Pallas kernels, device_fn(): pl.pallas_call(functools.partial(step_kernel, chips), out_shape=jax.Shape...  276 us
    pallas_call x1, Pallas kernels, device_fn(): pl.pallas_call(project_kernel, grid=(rows,), out_shape=(jax.ShapeDtypeStr...  13.8 us
    unnamed x16, local copies, waits for them, and re-layouts  6.38 us

profile of v2, /device:TPU:21, one launch (start us, length us, event | category | flops | bytes accessed | tf_op | source)
XLA Modules:
  0.0 312.6 jit_solution(11967487871626433656)
XLA Ops:
  0.0 0.8 fusion.1
  0.8 0.8 reshape.113
  1.5 0.7 copy.40
  2.2 0.7 copy.41
  2.8 0.7 copy.42
  3.5 1.4 concatenate.19
  4.9 0.8 broadcast_in_dim.17.bias_ref
  5.7 5.6 %copy.57 = bf16[512,16,256]{2,0,1:T(8,128)(2,1)} copy(bf16[512,16,256]{2,1,0:T(8,128)(2,1)} %param.18) | data formatting | bytes 8388608 | tf_op args[2]
  11.3 0.6 convert_element_type.15.norm_ref
  11.9 13.8 %project.1 = (bf16[2,16,32,512]{3,2,1,0:T(8,128)(2,1)}, bf16[2,512,512]{2,1,0:T(8,128)(2,1)}) custom-call(bf16[16,512,256]{2,1,0:T(8,128)(2,1)} %bitcast.34, bf16[2,64,256]{2,1,0:T(8,128)(2,1)} %bitcast.45, f32[2,2,256]{2,1,0:T(2,128)} %convert_element_type.15.norm_ref, f32[2,128,128]{2,1,0:T(8,128)} %broadcast_in_dim.17.bias_ref), custom_call_target="tpu_custom_call" | custom-call | tf_op jit(solution)/shard_map/project/pallas_call | solution.py:407
  25.7 1.6 broadcast_in_dim.19.vec_ref
  27.3 0.2 fusion
  27.6 0.4 maximum_bitcast_fusion
  28.1 1.0 copy.48
  29.1 0.3 copy.44
  29.4 1.3 copy.50.z_hbm
  30.7 0.2 copy.46
  30.9 1.0 copy.51.wq_ref
  31.9 0.2 reshape.106
  32.2 0.7 reshape.107.mask_ref
  32.9 0.7 copy.49
  33.6 276.1 %layers.1 = bf16[2,8,128,256]{3,2,1,0:T(8,128)(2,1)} custom-call(bf16[2,512,512]{2,1,0:T(8,128)(2,1)} %bitcast.39, bf16[2,32,16,512]{3,2,1,0:T(8,128)(2,1)} %bitcast.40, bf16[2,8,128,256]{3,2,1,0:T(8,128)(2,1)} %copy.50.z_hbm, f32[2,8,1,256]{3,2,1,0:T(1,128)} %reshape.107.mask_ref, bf16[2,128,1024]{2,1,0:T(8,128)(2,1)} %copy.51.wq_ref, ...), custom_call_target="tpu_custom_call" | custom-call | tf_op jit(solution)/shard_map/layers/pallas_call | solution.py:426
  309.8 1.6 copy.52
  311.4 1.2 copy.53
  (19 shorter events, 0.2 us)
Async XLA Ops:
  5.7 5.6 %copy-start.6 = (bf16[2,2,256]{2,1,0:T(2,128)(2,1)S(1)}, bf16[2,2,256]{2,1,0:T(2,128)(2,1)}, u32[]{:S(2)}) copy-start(bf16[2,2,256]{2,1,0:T(2,128)(2,1)} %param.19) | copy-start | bytes 6148
  11.3 16.0 %copy-start.2 = (bf16[2,128,4,128]{3,2,1,0:T(4,128)(2,1)S(1)}, bf16[2,128,4,128]{3,2,1,0:T(4,128)(2,1)}, u32[]{:S(2)}) copy-start(bf16[2,128,4,128]{3,2,1,0:T(4,128)(2,1)} %param.25) | copy-start | bytes 786436
  11.3 16.2 %copy-start.3 = (bf16[2,128,128]{2,1,0:T(8,128)(2,1)S(1)}, bf16[2,128,128]{2,1,0:T(8,128)(2,1)}, u32[]{:S(2)}) copy-start(bf16[2,128,128]{2,1,0:T(8,128)(2,1)} %param.27) | copy-start | bytes 196612
  25.7 3.4 %copy-start = (bf16[16,256,128]{2,1,0:T(8,128)(2,1)S(1)}, bf16[16,256,128]{2,1,0:T(8,128)(2,1)}, u32[]{:S(2)}) copy-start(bf16[16,256,128]{2,1,0:T(8,128)(2,1)} %param.16) | copy-start | bytes 3145732
  25.7 5.0 %copy-start.1 = (bf16[2,1024,128]{2,1,0:T(8,128)(2,1)S(1)}, bf16[2,1024,128]{2,1,0:T(8,128)(2,1)}, u32[]{:S(2)}) copy-start(bf16[2,1024,128]{2,1,0:T(8,128)(2,1)} %param.22) | copy-start | bytes 1572868
  27.5 4.5 %copy-start.5 = (s32[16,256]{1,0:T(8,128)S(1)}, s32[16,256]{1,0:T(8,128)}, u32[]{:S(2)}) copy-start(s32[16,256]{1,0:T(8,128)} %param.17) | copy-start | bytes 49156
  27.6 5.3 %copy-start.4 = (bf16[2,128,128]{2,1,0:T(8,128)(2,1)S(1)}, bf16[2,128,128]{2,1,0:T(8,128)(2,1)}, u32[]{:S(2)}) copy-start(bf16[2,128,128]{2,1,0:T(8,128)(2,1)} %param.30) | copy-start | bytes 196612

commit v3 on v2

--- a/solution.py
+++ b/solution.py
@@ -1,4 +1,5 @@
 import functools
+import math
 
 import jax
 import jax.numpy as jnp
@@ -32,29 +33,58 @@
     return jnp.concatenate([x, x], axis=1)
 
 
-def project_kernel(m_ref, w_ref, norm_ref, bias_ref, a_ref, b_ref, scr):
-    r = pl.program_id(0)
-    layers, width = w_ref.shape[0], w_ref.shape[1] // 2
-    seqs, dim = m_ref.shape[1], m_ref.shape[2]
-    rows = b_ref.shape[1] // width
-    x = m_ref[0].astype(F32)
-    xc = x - jnp.sum(x, axis=1, keepdims=True) * (1.0 / dim)
-    var = jnp.sum(xc * xc, axis=1, keepdims=True) * (1.0 / dim)
-    xn = xc * lax.rsqrt(var + EPS)
-    for l in range(layers):
-        mn = (xn * norm_ref[l, 0:1] + norm_ref[l, 1:2]).astype(BF16)
-        out = lax.dot_general(w_ref[l], mn, NT, preferred_element_type=F32)
-        bias = bias_ref[l][: 2 * width]
-        for c in range(seqs // LANES):
-            part = out[:, c * LANES : (c + 1) * LANES] + bias
-            a_ref[l, 0, :, c * LANES : (c + 1) * LANES] = part[:width].astype(BF16)
-            scr[l, c, pl.ds(r, width, stride=rows), :] = part[width:]
-
-    @pl.when(r == pl.num_programs(0) - 1)
-    def _():
-        for l in range(layers):
-            for c in range(seqs // LANES):
-                b_ref[l, :, c * LANES : (c + 1) * LANES] = scr[l, c].astype(BF16)
+def project_rows(l, first, count, m_ref, w_ref, norm_ref, bias_ref, a_ref, b_out, xa, xb, scr):
+    width = w_ref.shape[1] // 2
+    dim = w_ref.shape[2]
+    rows = scr.shape[0] // width
+    depth = xa.shape[1] // rows
+    block = 16
+    scale, offset = norm_ref[l, 0:1].astype(F32), norm_ref[l, 1:2].astype(F32)
+
+    def chunk(t, _):
+        at = pl.ds(pl.multiple_of((first + t) * rows, rows), rows)
+        lanes = pl.ds(pl.multiple_of((first + t) * LANES, LANES), LANES)
+
+        for part, x_ref in enumerate((xa, xb)):
+            def normalize(s, _):
+                x = m_ref[pl.ds(part * depth + s * block, block), at, :].astype(F32).reshape(block * rows, dim)
+                xc = x - jnp.sum(x, axis=1, keepdims=True) * (1.0 / dim)
+                var = jnp.sum(xc * xc, axis=1, keepdims=True) * (1.0 / dim)
+                xn = xc * lax.rsqrt(var + EPS)
+                to = pl.ds(pl.multiple_of(s * block * rows, block * rows), block * rows)
+                for f in range(dim // LANES):
+                    x_ref[f, to, :] = xn[:, f * LANES : (f + 1) * LANES]
+                return 0
+
+            lax.fori_loop(0, depth // block, normalize, 0)
+
+        def residue(t2, _):
+            for u in range(2):
+                r = 2 * t2 + u
+                xn = jnp.concatenate(
+                    [jnp.concatenate([x_ref[f, pl.ds(r, depth, stride=rows), :] for x_ref in (xa, xb)], axis=0)
+                     for f in range(dim // LANES)], axis=1)
+                mn = (xn * scale + offset).astype(BF16)
+                out = lax.dot_general(w_ref[l], mn, NT, preferred_element_type=F32) + bias_ref[l]
+                a_ref[l, pl.ds(pl.multiple_of(r * width, width), width), lanes] = out[:width].astype(BF16)
+                scr[pl.ds(r, width, stride=rows), :] = out[width:]
+            return 0
+
+        lax.fori_loop(0, rows // 2, residue, 0)
+        b_out(l, lanes, scr[...].astype(BF16).reshape(width, rows, LANES))
+        return 0
+
+    lax.fori_loop(0, count, chunk, 0)
+
+
+def prepare_wq(l, raw_ref, tmp_ref, wq_ref):
+    cd = raw_ref.shape[0]
+    width = math.isqrt(cd)
+    tmp_ref[0, :, :] = raw_ref[...].astype(F32)
+    for g in range(cd // LANES):
+        per = LANES // width
+        w = jnp.concatenate([tmp_ref[0, pl.ds(g * per + d, width, stride=width), :] for d in range(per)], axis=0)
+        wq_ref[l, :, g * LANES : (g + 1) * LANES] = w.T.astype(BF16)
 
 
 def opm_half(l, h, a_ref, b_ref, wq_ref, vec_ref, z_ref, q_ref):
@@ -93,7 +123,7 @@
 
     def project(p, _):
         zn = norm_rows(z_ref[h, p].astype(F32), twice(vec_ref[l, V_NI0]), twice(vec_ref[l, V_NI1]))
-        mask = mask_ref[h, p]
+        mask = jnp.concatenate([mask_ref[h, pl.ds(p + e * pairs, 1), :] for e in range(2)], axis=1)
         at = pl.ds(pl.multiple_of(p * dim, dim), dim)
 
         def proj(q, v):
@@ -236,47 +266,118 @@
                 self.across(2 + 2 * (hop - 1) + side, self.chip, self.core, side if hop == last else None).wait_send()
 
 
-N_STREAMS = 12
-
-
-def step_kernel(chips, a_hbm, b_hbm, z_hbm, mask_ref, wq_ref, wall_ref, wo_ref, vec_ref, out_hbm,
-                b_buf, t_buf, a_ref, z_ref, at_ref, g_ref, q_scr, fa, fb,
-                ring_send, ring_recv, core_send, core_recv, local_sem):
+N_STREAMS = 14
+N_LOADS = 64
+
+
+def layers_kernel(chips, m_hbm, z_hbm, wq_hbm, wab_hbm, wgate_hbm, wout_hbm, w_in_ref, b_in_ref, opm_norm_ref, mask_in,
+                  bq_ref, norm_in_ref, b_ab_ref, b_gate_ref, norm_out_ref, b_o_ref, out_hbm,
+                  b_buf, t_buf, a_ref, z_ref, at_ref, g_ref, q_scr, fa, fb, b_scr, wq_ref, wall_ref, wo_ref, vec_ref,
+                  bias_ref, mask_ref, ring_send, ring_recv, core_send, core_recv, local_sem):
     me = lax.axis_index("dap")
     chip, core = me // 2, lax.rem(me, 2)
-    rows = b_hbm.shape[2]
+    rows, cols, dim = z_hbm.shape
+    seqs = m_hbm.shape[0]
+    layers = a_ref.shape[0]
+    pairs = rows // 2
+    half = cols // 2
     own = pl.ds(pl.multiple_of(chip * rows, rows), rows)
-    layers = b_hbm.shape[0]
-    dim = at_ref.shape[1]
-    half = z_ref.shape[3] // 2
 
     barrier = pltpu.get_barrier_semaphore()
     right, left = lax.rem(chip + 1, chips), lax.rem(chip + chips - 1, chips)
     for there in (right * 2 + core, left * 2 + core, chip * 2 + 1 - core):
         pl.semaphore_signal(barrier, inc=1, device_id={"dap": there}, device_id_type=pl.DeviceIdType.MESH)
 
-    loads = [pltpu.make_async_copy(b_hbm.at[l], b_buf.at[l, core, :, own, :], local_sem.at[l]) for l in range(layers)]
-    loads.append(pltpu.make_async_copy(a_hbm, a_ref, local_sem.at[2]))
-    loads.append(pltpu.make_async_copy(z_hbm, z_ref, local_sem.at[3]))
-    for load in loads:
-        load.start()
-    pl.semaphore_wait(barrier, 3)
+    used = [0]
+
+    def load(src, dst):
+        copy = pltpu.make_async_copy(src, dst, local_sem.at[used[0]])
+        used[0] += 1
+        copy.start()
+        return copy
+
+    m_ref = t_buf.at[layers - 1, 0]
+    z_raw = t_buf.at[layers - 1, 1]
+    chunks = seqs // LANES
+    m_loads = [load(m_hbm.at[pl.ds(a * LANES, LANES)], m_ref.at[:, pl.ds(a * rows, rows), :]) for a in range(chunks)]
+    z_loads = [load(z_hbm.at[:, pl.ds((2 * c + h) * rows, rows), :],
+                    z_raw.at[pl.ds(0, rows), pl.ds(c * rows, rows), pl.ds(h * dim, dim)])
+               for h in range(2) for c in range(chips)]
+    w_loads = []
+    for l in range(layers):
+        cd, ab = wq_hbm.shape[1], wab_hbm.shape[1]
+        lanes = pl.ds(0, dim)
+        w_loads.append(load(wq_hbm.at[l], q_scr.at[l, :, lanes]))
+        w_loads.append(load(wab_hbm.at[l], q_scr.at[2 + l, pl.ds(0, ab), lanes]))
+        w_loads.append(load(wgate_hbm.at[l], q_scr.at[4 + l, pl.ds(0, dim), lanes]))
+        w_loads.append(load(wout_hbm.at[l], q_scr.at[4 + l, pl.ds(dim, dim), lanes]))
 
     where = (chip, core, chips)
-
-    def stream(n, buf, color, lo, lanes):
-        sems = tuple(s.at[n] for s in (ring_send, ring_recv, core_send, core_recv))
+    count = [0]
+
+    def stream(buf, color, lo, lanes):
+        sems = tuple(s.at[count[0]] for s in (ring_send, ring_recv, core_send, core_recv))
+        count[0] += 1
         return Stream(buf, color, lo, lanes, rows, sems, where)
 
     width = b_buf.shape[2]
-    full_b = pl.ds(0, b_buf.shape[4])
-    full_t = pl.ds(0, 2 * half)
-    b1 = [stream(q, b_buf.at[0, q], q, (0, width // 2), full_b) for q in range(2)]
-    b2 = [stream(2 + q, b_buf.at[1, q], q, (0, width // 2), full_b) for q in range(2)]
-    t1 = [[stream(4 + 2 * q + s, t_buf.at[0, q], q, (s * dim // 4, dim // 4), full_t) for s in range(2)]
-          for q in range(2)]
-    t2 = [[stream(8 + 2 * k + q, t_buf.at[1, q], q, (0, dim // 2), pl.ds(k * half, half)) for q in range(2)]
-          for k in range(2)]
+    full_b = pl.ds(0, seqs)
+    full_t = pl.ds(0, cols)
+    b1 = [[stream(b_buf.at[0, q], q, (0, width // 2), pl.ds(s * (seqs // 2), seqs // 2)) for q in range(2)]
+          for s in range(2)]
+    b2 = [stream(b_buf.at[1, q], q, (0, width // 2), full_b) for q in range(2)]
+    t1 = [[stream(t_buf.at[0, q], q, (s * dim // 4, dim // 4), full_t) for s in range(2)] for q in range(2)]
+    t2 = [[stream(t_buf.at[1, q], q, (0, dim // 2), pl.ds(k * half, half)) for q in range(2)] for k in range(2)]
+
+    def column(row):
+        return jnp.broadcast_to(row, (LANES, row.shape[1])).T
+
+    for l in range(layers):
+        bias_ref[l] = column(b_in_ref[l])[: 2 * width]
+
+    def project(l, first, n):
+        def b_out(l, lanes, v):
+            b_buf[l, core, :, own, lanes] = v
+
+        project_rows(l, first, n, m_ref, w_in_ref, opm_norm_ref, bias_ref, a_ref, b_out, fa, fb, b_scr)
+
+    def vectors():
+        bq, b_gate, b_o = (r[...].astype(F32) for r in (bq_ref, b_gate_ref, b_o_ref))
+        for l in range(layers):
+            norm_in, b_ab, norm_out = (r[l].astype(F32) for r in (norm_in_ref, b_ab_ref, norm_out_ref))
+            table = ((V_BQ, bq, l), (V_BP, b_ab, 2), (V_BG, b_ab, 3), (V_AP, b_ab, 0), (V_AG, b_ab, 1),
+                     (V_GATE, b_gate, l), (V_NI0, norm_in, 0), (V_NI1, norm_in, 1), (V_NO0, norm_out, 0),
+                     (V_NO1, norm_out, 1), (V_BO, b_o, l))
+            for v, src, r in table:
+                vec_ref[l, v] = column(src[r : r + 1])
+
+    def masks():
+        to = lax.broadcasted_iota(jnp.int32, (cols, cols), 1)
+        frm = lax.broadcasted_iota(jnp.int32, (cols, cols), 0)
+        q, rest = to // half, to % half
+        perm = (frm == (rest // rows) * (2 * rows) + q * rows + rest % rows).astype(F32).astype(BF16)
+        mask = jnp.dot(mask_in[...].astype(F32).astype(BF16), perm, preferred_element_type=F32)
+        for h in range(2):
+            mask_ref[h] = mask[:, h * half : (h + 1) * half]
+
+    def weights(l):
+        prepare_wq(l, q_scr.at[l, :, pl.ds(0, dim)], fa, wq_ref)
+        ab = wab_hbm.shape[1]
+        fa[0, 0:ab, :] = q_scr[2 + l, 0:ab, 0:dim].astype(F32)
+        for slot, q in enumerate((2, 3, 0, 1)):
+            wall_ref[l, slot * dim : (slot + 1) * dim, :] = fa[0, pl.ds(q, dim, stride=4), :].T.astype(BF16)
+        wall_ref[l, 4 * dim : 5 * dim, :] = q_scr[4 + l, 0:dim, 0:dim].astype(F32).T.astype(BF16)
+        wo_ref[l] = q_scr[4 + l, dim : 2 * dim, 0:dim].astype(F32).T.astype(BF16)
+
+    def pair_in():
+        def step(p, _):
+            for h in range(2):
+                for e in range(2):
+                    x = z_raw[e * pairs + p, :, h * dim : (h + 1) * dim].astype(F32)
+                    z_ref[h, p, :, e * half : (e + 1) * half] = x.T.astype(BF16)
+            return 0
+
+        lax.fori_loop(0, pairs, step, 0)
 
     def opm(l, h):
         opm_half(l, h, a_ref, b_buf.at[l], wq_ref, vec_ref, z_ref, q_scr)
@@ -296,24 +397,57 @@
     def finish(l, jh):
         finish_half(l, jh, fa, g_ref, z_ref, wo_ref, vec_ref)
 
+    def pair_out(h):
+        def step(p, _):
+            for e in range(2):
+                x = z_ref[h, p, :, e * half : (e + 1) * half].astype(F32)
+                q_scr[p, h * half : (h + 1) * half, e * dim : (e + 1) * dim] = x.T.astype(BF16)
+            return 0
+
+        lax.fori_loop(0, pairs, step, 0)
+        return [load(q_scr.at[:, pl.ds(h * half + c * rows, rows), pl.ds(e * dim, dim)],
+                     out_hbm.at[pl.ds(e * pairs, pairs), pl.ds((2 * c + h) * rows, rows), :])
+                for e in range(2) for c in range(chips)]
+
     def events(hop, *streams):
         for s in streams:
             s.event(hop)
 
-    loads[0].wait()
-    events(0, *b1)
-    loads[1].wait()
-    events(1, *b1)
-    events(2, *b1)
-    loads[2].wait()
-    loads[3].wait()
-    events(3, *b1)
+    def wait(copies):
+        for copy in copies:
+            copy.wait()
+
+    wait(m_loads[: chunks // 2])
+    project(0, 0, chunks // 2)
+    pl.semaphore_wait(barrier, 3)
+    events(0, *b1[0])
+    wait(m_loads[chunks // 2 :])
+    project(0, chunks // 2, chunks // 2)
+    vectors()
+    events(0, *b1[1])
+    events(1, *b1[0])
+    events(1, *b1[1])
+    wait(w_loads)
+    weights(0)
+    events(2, *b1[0])
+    masks()
+    wait(z_loads)
+    pair_in()
+    events(2, *b1[1])
+    project(1, 0, chunks // 2)
+    events(3, *b1[0])
+    project(1, chunks // 2, chunks // 2)
+    events(3, *b1[1])
+    weights(1)
     events(0, *b2)
-    events(4, *b1)
-    b1[0].finish()
+    events(4, *b1[0])
+    events(4, *b1[1])
+    for s in range(2):
+        b1[s][0].finish()
     opm(0, 0)
     events(1, b2[0])
-    b1[1].finish()
+    for s in range(2):
+        b1[s][1].finish()
     opm(0, 1)
     events(1, b2[1])
     gate(0, 0)
@@ -357,22 +491,22 @@
     events(2, *t2[1])
     events(3, *t2[1])
     events(4, *t2[1])
+    stores = []
     for q in range(2):
         t2[0][q].finish()
         t2[1][q].finish()
         triangle(1, q)
         finish(1, q)
-        store = pltpu.make_async_copy(z_ref.at[q], out_hbm.at[q], local_sem.at[q])
-        store.start()
-    for s in b1 + b2 + t1[0] + t1[1] + t2[0] + t2[1]:
+        stores += pair_out(q)
+    for s in b1[0] + b1[1] + b2 + t1[0] + t1[1] + t2[0] + t2[1]:
         s.drain()
-    for q in range(2):
-        pltpu.make_async_copy(z_ref.at[q], out_hbm.at[q], local_sem.at[q]).wait()
+    wait(stores)
 
 
 def solution(mesh):
     size = mesh.shape["dap"]
     chips = size // 2
+    hops = chips // 2
     pair_spec = P(("batch", "dap"), None, None)
     mask_spec = P(("batch", "dap"), None)
     msa_spec = P(None, ("batch", "dap"), None)
@@ -387,66 +521,42 @@
         width = opm_w_in.shape[-1]
         pairs = rows // 2
         half = cols // 2
+        z_shape = (2, pairs, dim, 2 * half)
 
         w_in = jnp.transpose(opm_w_in, (0, 2, 3, 1)).reshape(layers, 2 * width, mdim)
-        wq = jnp.transpose(opm_w_out.reshape(layers, width, width, dim), (0, 3, 2, 1)).reshape(layers, dim, -1)
-        w5 = jnp.concatenate([tri_w_ab[:, :, 2:4], tri_w_ab[:, :, 0:2], tri_w_gate[:, :, None]], axis=2)
-        wall = jnp.transpose(w5, (0, 2, 3, 1)).reshape(layers, 5 * dim, dim)
-        wo = jnp.transpose(tri_w_out, (0, 2, 1))
-        b_in = jnp.pad(opm_b_in.reshape(layers, 1, 2 * width), ((0, 0), (0, 0), (0, dim - 2 * width)))
-        vec = jnp.concatenate([opm_b_out[:, None], tri_b_ab[:, 2:4], tri_b_ab[:, 0:2], tri_b_gate[:, None],
-                               tri_norm_in, tri_norm_out, tri_b_out[:, None], b_in], axis=1).astype(F32)
-        vec = jnp.broadcast_to(vec[..., None], vec.shape + (LANES,))
-
-        z = pair_act.reshape(2, pairs, chips, 2, rows, dim)
-        z = jnp.transpose(z, (3, 1, 5, 0, 2, 4)).reshape(2, pairs, dim, 2 * half)
-        mask = pair_mask.astype(F32).reshape(2, pairs, chips, 2, rows)
-        mask = jnp.transpose(mask, (3, 1, 0, 2, 4)).reshape(2, pairs, 1, 2 * half)
-        m = jnp.swapaxes(msa_act, 0, 1)
-
-        a, b = pl.pallas_call(
-            project_kernel,
-            grid=(rows,),
-            out_shape=(jax.ShapeDtypeStruct((layers, rows, width, seqs), BF16),
-                       jax.ShapeDtypeStruct((layers, width * rows, seqs), BF16)),
-            in_specs=[pl.BlockSpec((1, seqs, mdim), lambda r: (r, 0, 0)),
-                      pl.BlockSpec(w_in.shape, lambda r: (0, 0, 0)),
-                      pl.BlockSpec(opm_norm.shape, lambda r: (0, 0, 0)),
-                      pl.BlockSpec((layers, dim, LANES), lambda r: (0, 0, 0))],
-            out_specs=(pl.BlockSpec((layers, 1, width, seqs), lambda r: (0, r, 0, 0)),
-                       pl.BlockSpec((layers, width * rows, seqs), lambda r: (0, 0, 0))),
-            scratch_shapes=[pltpu.VMEM((layers, seqs // LANES, width * rows, LANES), F32)],
-            compiler_params=pltpu.CompilerParams(vmem_limit_bytes=VMEM_LIMIT),
-            name="project",
-        )(m, w_in, opm_norm.astype(F32), vec[:, V_BIN])
-        a = a.reshape(layers, rows * width, seqs)
-        b = b.reshape(layers, width, rows, seqs)
-
-        hops = chips // 2
-        z = pl.pallas_call(
-            functools.partial(step_kernel, chips),
-            out_shape=jax.ShapeDtypeStruct(z.shape, BF16),
-            in_specs=[any_spec] * 3 + [vmem_spec] * 5,
+        b_in = jnp.pad(opm_b_in.reshape(layers, 1, 2 * width), ((0, 0), (0, 0), (0, dim - 2 * width))).astype(F32)
+        w_ab = tri_w_ab.reshape(layers, dim * 4, dim)
+
+        return pl.pallas_call(
+            functools.partial(layers_kernel, chips),
+            out_shape=jax.ShapeDtypeStruct(pair_act.shape, BF16),
+            in_specs=[any_spec] * 6 + [vmem_spec] * 10,
             out_specs=any_spec,
             scratch_shapes=[pltpu.VMEM((layers, 2, width, half, seqs), BF16),
                             pltpu.VMEM((layers, 2, dim, half, cols), BF16),
-                            pltpu.VMEM(a.shape, BF16),
-                            pltpu.VMEM(z.shape, BF16),
+                            pltpu.VMEM((layers, rows * width, seqs), BF16),
+                            pltpu.VMEM(z_shape, BF16),
                             pltpu.VMEM((layers, dim, rows, cols), BF16),
-                            pltpu.VMEM(z.shape, F32),
+                            pltpu.VMEM(z_shape, F32),
                             pltpu.VMEM((pairs, width * width, 2 * half), BF16),
                             pltpu.VMEM((2, pairs * dim, LANES), F32),
                             pltpu.VMEM((2, pairs * dim, LANES), F32),
+                            pltpu.VMEM((width * rows, LANES), F32),
+                            pltpu.VMEM((layers, dim, width * width), BF16),
+                            pltpu.VMEM((layers, 5 * dim, dim), BF16),
+                            pltpu.VMEM((layers, dim, dim), BF16),
+                            pltpu.VMEM((layers, V_BIN, dim, LANES), F32),
+                            pltpu.VMEM((layers, 2 * width, LANES), F32),
+                            pltpu.VMEM((2, rows, half), F32),
                             pltpu.SemaphoreType.DMA((N_STREAMS, 2, hops)),
                             pltpu.SemaphoreType.DMA((N_STREAMS, 2, hops)),
                             pltpu.SemaphoreType.DMA((N_STREAMS, 2 + 2 * hops)),
                             pltpu.SemaphoreType.DMA((N_STREAMS, 2 + 2 * hops)),
-                            pltpu.SemaphoreType.DMA((4,))],
+                            pltpu.SemaphoreType.DMA((N_LOADS,))],
             compiler_params=pltpu.CompilerParams(vmem_limit_bytes=VMEM_LIMIT, collective_id=0, has_side_effects=True),
             name="layers",
-        )(a, b, z, mask, wq, wall, wo, vec)
-        out = z.reshape(2, pairs, dim, 2, chips, rows)
-        return jnp.transpose(out, (3, 1, 4, 0, 5, 2)).reshape(rows, cols, dim)
+        )(msa_act, pair_act, opm_w_out, w_ab, tri_w_gate, tri_w_out, w_in, b_in, opm_norm, pair_mask,
+          opm_b_out, tri_norm_in, tri_b_ab, tri_b_gate, tri_norm_out, tri_b_out)
 
     return jax.shard_map(device_fn, mesh=mesh, in_specs=(pair_spec, mask_spec, msa_spec) + (P(),) * 13,
                          out_specs=pair_spec, check_vma=False)

time: 313 us -> 296 us (0.946)
  local copies, waits for them, and re-layouts: 21.5 us -> 3.06 us
    unnamed x16 -> x1, local copies, waits for them, and re-layouts: 6.38 us -> 2.3 us
    concatenate x4 -> x0, local copies, waits for them, and re-layouts: 3.38 us -> none  [device_fn(): jnp.concatenate([opm_b_out[:, None], tri_b_ab[:, 2:4], tri_b_ab[:, 0:2],...]
    reshape x5 -> x0, local copies, waits for them, and re-layouts: 3.26 us -> none  [the longest x1 1.33 us: device_fn(): z = jnp.transpose(z, (3, 1, 5, 0, 2, 4)).reshape(2, pairs, dim, 2 * half)]
    pallas_call x2 -> x1, Pallas kernels: 290 us -> 292 us  [device_fn(): pl.pallas_call(functools.partial(layers_kernel, chips), out_shape=jax.Sha...]
where the time goes in v3:
time: 296 us
  Pallas kernels  292 us (99%)
  local copies, waits for them, and re-layouts  3.06 us (1%)
    pallas_call x1, Pallas kernels, device_fn(): pl.pallas_call(functools.partial(layers_kernel, chips), out_shape=jax.Sha...  292 us

profile of v3, /device:TPU:21, one launch (start us, length us, event | category | flops | bytes accessed | tf_op | source)
XLA Modules:
  0.0 295.9 jit_solution(3416187501775727112)
XLA Ops:
  0.0 0.8 reshape.12
  0.8 0.6 pad_convert_fusion.b_in_ref
  1.3 292.3 %layers.1 = bf16[16,256,128]{2,1,0:T(8,128)(2,1)} custom-call(bf16[512,16,256]{2,1,0:T(8,128)(2,1)} %m_hbm.1, bf16[16,256,128]{2,1,0:T(8,128)(2,1)} %z_hbm.1, bf16[2,1024,128]{2,1,0:T(8,128)(2,1)} %wq_hbm.1, bf16[2,512,128]{2,1,0:T(8,128)(2,1)} %bitcast.4, bf16[2,128,128]{2,1,0:T(8,128)(2,1)} %wgate_hbm.1, bf16[2,128,128]{2,1,0:T(8,128)(2,1)} %wout_hbm.1, ...), custom_call_target="tpu_custom_call" | custom-call | tf_op jit(solution)/shard_map/layers/pallas_call | solution.py:530
  293.6 2.3 copy.19

commit v4 on v3

--- a/solution.py
+++ b/solution.py
@@ -33,7 +33,7 @@
     return jnp.concatenate([x, x], axis=1)
 
 
-def project_rows(l, first, count, m_ref, w_ref, norm_ref, bias_ref, a_ref, b_out, xa, xb, scr):
+def project_rows(l, chunk, m_ref, w_ref, norm_ref, bias_ref, a_ref, b_out, xa, xb, scr):
     width = w_ref.shape[1] // 2
     dim = w_ref.shape[2]
     rows = scr.shape[0] // width
@@ -41,40 +41,36 @@
     block = 16
     scale, offset = norm_ref[l, 0:1].astype(F32), norm_ref[l, 1:2].astype(F32)
 
-    def chunk(t, _):
-        at = pl.ds(pl.multiple_of((first + t) * rows, rows), rows)
-        lanes = pl.ds(pl.multiple_of((first + t) * LANES, LANES), LANES)
-
-        for part, x_ref in enumerate((xa, xb)):
-            def normalize(s, _):
-                x = m_ref[pl.ds(part * depth + s * block, block), at, :].astype(F32).reshape(block * rows, dim)
-                xc = x - jnp.sum(x, axis=1, keepdims=True) * (1.0 / dim)
-                var = jnp.sum(xc * xc, axis=1, keepdims=True) * (1.0 / dim)
-                xn = xc * lax.rsqrt(var + EPS)
-                to = pl.ds(pl.multiple_of(s * block * rows, block * rows), block * rows)
-                for f in range(dim // LANES):
-                    x_ref[f, to, :] = xn[:, f * LANES : (f + 1) * LANES]
-                return 0
-
-            lax.fori_loop(0, depth // block, normalize, 0)
-
-        def residue(t2, _):
-            for u in range(2):
-                r = 2 * t2 + u
-                xn = jnp.concatenate(
-                    [jnp.concatenate([x_ref[f, pl.ds(r, depth, stride=rows), :] for x_ref in (xa, xb)], axis=0)
-                     for f in range(dim // LANES)], axis=1)
-                mn = (xn * scale + offset).astype(BF16)
-                out = lax.dot_general(w_ref[l], mn, NT, preferred_element_type=F32) + bias_ref[l]
-                a_ref[l, pl.ds(pl.multiple_of(r * width, width), width), lanes] = out[:width].astype(BF16)
-                scr[pl.ds(r, width, stride=rows), :] = out[width:]
+    at = pl.ds(chunk * rows, rows)
+    lanes = pl.ds(chunk * LANES, LANES)
+
+    for part, x_ref in enumerate((xa, xb)):
+        def normalize(s, _):
+            x = m_ref[pl.ds(part * depth + s * block, block), at, :].astype(F32).reshape(block * rows, dim)
+            xc = x - jnp.sum(x, axis=1, keepdims=True) * (1.0 / dim)
+            var = jnp.sum(xc * xc, axis=1, keepdims=True) * (1.0 / dim)
+            xn = xc * lax.rsqrt(var + EPS)
+            to = pl.ds(pl.multiple_of(s * block * rows, block * rows), block * rows)
+            for f in range(dim // LANES):
+                x_ref[f, to, :] = xn[:, f * LANES : (f + 1) * LANES]
             return 0
 
-        lax.fori_loop(0, rows // 2, residue, 0)
-        b_out(l, lanes, scr[...].astype(BF16).reshape(width, rows, LANES))
+        lax.fori_loop(0, depth // block, normalize, 0)
+
+    def residue(t2, _):
+        for u in range(2):
+            r = 2 * t2 + u
+            xn = jnp.concatenate(
+                [jnp.concatenate([x_ref[f, pl.ds(r, depth, stride=rows), :] for x_ref in (xa, xb)], axis=0)
+                 for f in range(dim // LANES)], axis=1)
+            mn = (xn * scale + offset).astype(BF16)
+            out = lax.dot_general(w_ref[l], mn, NT, preferred_element_type=F32) + bias_ref[l]
+            a_ref[l, pl.ds(pl.multiple_of(r * width, width), width), lanes] = out[:width].astype(BF16)
+            scr[pl.ds(r, width, stride=rows), :] = out[width:]
         return 0
 
-    lax.fori_loop(0, count, chunk, 0)
+    lax.fori_loop(0, rows // 2, residue, 0)
+    b_out(l, lanes, scr[...].astype(BF16).reshape(width, rows, LANES))
 
 
 def prepare_wq(l, raw_ref, tmp_ref, wq_ref):
@@ -87,7 +83,7 @@
         wq_ref[l, :, g * LANES : (g + 1) * LANES] = w.T.astype(BF16)
 
 
-def opm_half(l, h, a_ref, b_ref, wq_ref, vec_ref, z_ref, q_ref):
+def outer_half(l, h, part, parts, a_ref, b_ref, q_ref):
     pairs, cd, lanes2 = q_ref.shape
     seqs = a_ref.shape[2]
     width = a_ref.shape[1] // (2 * pairs)
@@ -105,7 +101,12 @@
                 q_ref[:, at, e * half : (e + 1) * half] = blk[e * pairs : (e + 1) * pairs]
         return 0
 
-    lax.fori_loop(0, cd // width // 2, outer, 0)
+    steps = cd // width // 2 // parts
+    lax.fori_loop(part * steps, (part + 1) * steps, outer, 0)
+
+
+def opm_half(l, h, wq_ref, vec_ref, z_ref, q_ref):
+    pairs = q_ref.shape[0]
     bq = twice(vec_ref[l, V_BQ])
 
     def project(p, _):
@@ -151,14 +152,14 @@
         lax.fori_loop(0, dim // 8, relayout, 0)
 
 
-def triangle_half(jh, a_ref, b_ref, o_ref):
+def triangle_half(jh, k, a_ref, b_ref, o_ref):
     dim = a_ref.shape[0]
     pairs = a_ref.shape[1] // 2
 
     def step(t, _):
         for u in range(8):
             c = t * 8 + u
-            o = lax.dot_general(a_ref[c], b_ref[jh, c], NT, preferred_element_type=F32)
+            o = lax.dot_general(a_ref[c, :, k], b_ref[jh, c, :, k], NT, preferred_element_type=F32)
             o_ref[0, pl.ds(c, pairs, stride=dim), :] = o[:pairs]
             o_ref[1, pl.ds(c, pairs, stride=dim), :] = o[pairs:]
         return 0
@@ -166,13 +167,13 @@
     lax.fori_loop(0, dim // 8, step, 0)
 
 
-def finish_half(l, jh, o_ref, g_ref, z_ref, wo_ref, vec_ref):
+def finish_half(l, jh, o_refs, g_ref, z_ref, wo_ref, vec_ref):
     pairs = z_ref.shape[1]
     dim = z_ref.shape[2]
 
     def step(p, _):
         at = pl.ds(pl.multiple_of(p * dim, dim), dim)
-        o = jnp.concatenate([o_ref[0, at, :], o_ref[1, at, :]], axis=1)
+        o = sum(jnp.concatenate([o_ref[0, at, :], o_ref[1, at, :]], axis=1) for o_ref in o_refs)
         on = norm_rows(o, twice(vec_ref[l, V_NO0]), twice(vec_ref[l, V_NO1]))
         u = jnp.dot(wo_ref[l], on, preferred_element_type=F32) + twice(vec_ref[l, V_BO])
         z_ref[jh, p] = (z_ref[jh, p].astype(F32) + g_ref[jh, p] * u.astype(BF16).astype(F32)).astype(BF16)
@@ -215,14 +216,15 @@
                          self.chip, 1 - self.core)
 
     def event(self, hop):
-        if hop == 0:
+        if hop == -1:
             @pl.when(self.core == self.color)
             def _():
                 self.across(0, self.chip, 1 - self.core).start()
                 for side in range(2):
                     self.ring(side, 0, self.chip).start()
                 self.across(1, self.chip, self.core).start()
-
+            return
+        if hop == 0:
             @pl.when(self.core != self.color)
             def _():
                 self.across(0, self.chip, self.core).wait_recv()
@@ -266,8 +268,36 @@
                 self.across(2 + 2 * (hop - 1) + side, self.chip, self.core, side if hop == last else None).wait_send()
 
 
-N_STREAMS = 14
-N_LOADS = 64
+ORDER = (
+    "p0", ("b100", -1), ("b101", -1), "p1", ("b100", 0), ("b101", 0), ("b110", -1), ("b111", -1), "p2", ("b110", 0),
+    ("b111", 0), "p3", ("b120", -1), ("b121", -1), ("b100", 1), ("b101", 1), "vec", ("b120", 0), ("b121", 0), "w0",
+    ("b110", 1), ("b111", 1), "mask", "pin", "q0", ("b100", 2), "q1", ("b101", 2), "q2", ("b120", 1), ("b121", 1),
+    "q3", ("b110", 2), ("b111", 2), "w1", ("b100", 3), ("b101", 3), ("b120", 2), ("b121", 2), ("b110", 3),
+    ("b111", 3), ("b100", 4), ("b101", 4), ("b20", -1), ("b20", 0), ("b120", 3), ("b121", 3), ("b110", 4),
+    ("b111", 4), ("b21", -1), ("b21", 0), ("b20", 1), ("b120", 4), ("b121", 4), "O00a", "O00b", ("b21", 1), "O00p",
+    "G00", ("b20", 2), "O01a", "O01b", ("b21", 2), "O01p", "G01", ("t100", -1), ("b20", 3), ("t101", -1),
+    ("t100", 0), ("b21", 3), ("t101", 0), ("t100", 1), ("b20", 4), ("b21", 4), ("t101", 1), ("t100", 2),
+    ("t101", 2), ("t100", 3), ("t110", -1), ("t110", 0), ("t101", 3), ("t100", 4), ("t111", -1), ("t111", 0),
+    ("t110", 1), ("t101", 4), "T00", ("t111", 1), "N00", "O10a", "O10b", ("t110", 2), "O10p", "G10", ("t111", 2),
+    ("t200", -1), ("t201", -1), ("t200", 0), ("t201", 0), ("t110", 3), ("t111", 3), ("t200", 1), ("t201", 1),
+    ("t110", 4), ("t111", 4), "T01", ("t200", 2), "N01", "O11a", "O11b", ("t201", 2), "O11p", "G11", ("t210", -1),
+    ("t200", 3), ("t210", 0), ("t201", 3), ("t211", -1), ("t211", 0), ("t210", 1), ("t200", 4), ("t201", 4), "K1",
+    ("t211", 1), ("t210", 2), ("t211", 2), ("t210", 3), ("t211", 3), ("t210", 4), "T10", ("t211", 4), "N10", "X10",
+    "L1", "N11", "X11",
+)
+NEEDS = {
+    "O00a": ("b100", "b110", "b120",),
+    "O01a": ("b101", "b111", "b121",),
+    "T00": ("t100", "t101",),
+    "O10a": ("b20",),
+    "T01": ("t110", "t111",),
+    "O11a": ("b21",),
+    "K1": ("t201",),
+    "T10": ("t200", "t210",),
+    "L1": ("t211",),
+}
+N_STREAMS = 16
+N_LOADS = 32
 
 
 def layers_kernel(chips, m_hbm, z_hbm, wq_hbm, wab_hbm, wgate_hbm, wout_hbm, w_in_ref, b_in_ref, opm_norm_ref, mask_in,
@@ -291,7 +321,7 @@
     used = [0]
 
     def load(src, dst):
-        copy = pltpu.make_async_copy(src, dst, local_sem.at[used[0]])
+        copy = pltpu.make_async_copy(src, dst, local_sem.at[used[0] % N_LOADS])
         used[0] += 1
         copy.start()
         return copy
@@ -323,11 +353,15 @@
     width = b_buf.shape[2]
     full_b = pl.ds(0, seqs)
     full_t = pl.ds(0, cols)
-    b1 = [[stream(b_buf.at[0, q], q, (0, width // 2), pl.ds(s * (seqs // 2), seqs // 2)) for q in range(2)]
-          for s in range(2)]
-    b2 = [stream(b_buf.at[1, q], q, (0, width // 2), full_b) for q in range(2)]
-    t1 = [[stream(t_buf.at[0, q], q, (s * dim // 4, dim // 4), full_t) for s in range(2)] for q in range(2)]
-    t2 = [[stream(t_buf.at[1, q], q, (0, dim // 2), pl.ds(k * half, half)) for q in range(2)] for k in range(2)]
+    named = {}
+    for s, (lo, n) in enumerate(((0, 1), (1, 1), (2, chunks - 2))):
+        for q in range(2):
+            named[f"b1{s}{q}"] = stream(b_buf.at[0, q], q, (0, width // 2), pl.ds(lo * LANES, n * LANES))
+    for q in range(2):
+        named[f"b2{q}"] = stream(b_buf.at[1, q], q, (0, width // 2), full_b)
+        for s in range(2):
+            named[f"t1{q}{s}"] = stream(t_buf.at[0, q], q, (s * dim // 4, dim // 4), full_t)
+            named[f"t2{s}{q}"] = stream(t_buf.at[1, q], q, (0, dim // 2), pl.ds(s * half, half))
 
     def column(row):
         return jnp.broadcast_to(row, (LANES, row.shape[1])).T
@@ -335,11 +369,11 @@
     for l in range(layers):
         bias_ref[l] = column(b_in_ref[l])[: 2 * width]
 
-    def project(l, first, n):
+    def project(l, chunk):
         def b_out(l, lanes, v):
             b_buf[l, core, :, own, lanes] = v
 
-        project_rows(l, first, n, m_ref, w_in_ref, opm_norm_ref, bias_ref, a_ref, b_out, fa, fb, b_scr)
+        project_rows(l, chunk, m_ref, w_in_ref, opm_norm_ref, bias_ref, a_ref, b_out, fa, fb, b_scr)
 
     def vectors():
         bq, b_gate, b_o = (r[...].astype(F32) for r in (bq_ref, b_gate_ref, b_o_ref))
@@ -379,8 +413,11 @@
 
         lax.fori_loop(0, pairs, step, 0)
 
+    def outer(l, h, part):
+        outer_half(l, h, part, 2, a_ref, b_buf.at[l], q_scr)
+
     def opm(l, h):
-        opm_half(l, h, a_ref, b_buf.at[l], wq_ref, vec_ref, z_ref, q_scr)
+        opm_half(l, h, wq_ref, vec_ref, z_ref, q_scr)
 
     def gate(l, h):
         def a_out(c, h, v):
@@ -391,11 +428,11 @@
 
         gate_half(l, h, z_ref, mask_ref, wall_ref, vec_ref, fa, fb, g_ref, a_out, b_out)
 
-    def triangle(l, jh):
-        triangle_half(jh, at_ref.at[l], t_buf.at[l], fa)
-
-    def finish(l, jh):
-        finish_half(l, jh, fa, g_ref, z_ref, wo_ref, vec_ref)
+    def triangle(l, jh, k=full_t, o_ref=fa):
+        triangle_half(jh, k, at_ref.at[l], t_buf.at[l], o_ref)
+
+    def finish(l, jh, *o_refs):
+        finish_half(l, jh, o_refs or (fa,), g_ref, z_ref, wo_ref, vec_ref)
 
     def pair_out(h):
         def step(p, _):
@@ -409,98 +446,53 @@
                      out_hbm.at[pl.ds(e * pairs, pairs), pl.ds((2 * c + h) * rows, rows), :])
                 for e in range(2) for c in range(chips)]
 
-    def events(hop, *streams):
-        for s in streams:
-            s.event(hop)
-
-    def wait(copies):
-        for copy in copies:
+    stores = []
+
+    def first_project(chunk):
+        m_loads[chunk].wait()
+        project(0, chunk)
+        if chunk == 0:
+            pl.semaphore_wait(barrier, 3)
+
+    def first_weights():
+        for copy in w_loads:
             copy.wait()
-
-    wait(m_loads[: chunks // 2])
-    project(0, 0, chunks // 2)
-    pl.semaphore_wait(barrier, 3)
-    events(0, *b1[0])
-    wait(m_loads[chunks // 2 :])
-    project(0, chunks // 2, chunks // 2)
-    vectors()
-    events(0, *b1[1])
-    events(1, *b1[0])
-    events(1, *b1[1])
-    wait(w_loads)
-    weights(0)
-    events(2, *b1[0])
-    masks()
-    wait(z_loads)
-    pair_in()
-    events(2, *b1[1])
-    project(1, 0, chunks // 2)
-    events(3, *b1[0])
-    project(1, chunks // 2, chunks // 2)
-    events(3, *b1[1])
-    weights(1)
-    events(0, *b2)
-    events(4, *b1[0])
-    events(4, *b1[1])
-    for s in range(2):
-        b1[s][0].finish()
-    opm(0, 0)
-    events(1, b2[0])
-    for s in range(2):
-        b1[s][1].finish()
-    opm(0, 1)
-    events(1, b2[1])
-    gate(0, 0)
-    events(2, b2[0])
-    gate(0, 1)
-    events(2, b2[1])
-    events(0, *t1[0])
-    events(3, *b2)
-    events(1, *t1[0])
-    events(4, *b2)
-    events(2, *t1[0])
-    events(0, *t1[1])
-    events(3, *t1[0])
-    events(4, *t1[0])
-    for s in t1[0]:
-        s.finish()
-    triangle(0, 0)
-    events(1, *t1[1])
-    finish(0, 0)
-    events(2, t1[1][0])
-    for s in b2:
-        s.finish()
-    opm(1, 0)
-    events(2, t1[1][1])
-    events(3, *t1[1])
-    gate(1, 0)
-    events(0, *t2[0])
-    events(4, *t1[1])
-    for s in t1[1]:
-        s.finish()
-    triangle(0, 1)
-    finish(0, 1)
-    events(1, *t2[0])
-    opm(1, 1)
-    events(2, *t2[0])
-    gate(1, 1)
-    events(0, *t2[1])
-    events(3, *t2[0])
-    events(1, *t2[1])
-    events(4, *t2[0])
-    events(2, *t2[1])
-    events(3, *t2[1])
-    events(4, *t2[1])
-    stores = []
-    for q in range(2):
-        t2[0][q].finish()
-        t2[1][q].finish()
-        triangle(1, q)
-        finish(1, q)
-        stores += pair_out(q)
-    for s in b1[0] + b1[1] + b2 + t1[0] + t1[1] + t2[0] + t2[1]:
+        weights(0)
+
+    def first_pairs():
+        for copy in z_loads:
+            copy.wait()
+        pair_in()
+
+    tasks = {"vec": vectors, "mask": masks, "w0": first_weights, "w1": lambda: weights(1), "pin": first_pairs,
+             "K1": lambda: triangle(1, 1, pl.ds(0, half), fb), "L1": lambda: triangle(1, 1, pl.ds(half, half), fa),
+             "N11": lambda: finish(1, 1, fa, fb)}
+    for c in range(chunks):
+        tasks[f"p{c}"] = functools.partial(first_project, c)
+        tasks[f"q{c}"] = functools.partial(project, 1, c)
+    for l in range(layers):
+        for h in range(2):
+            for part, letter in enumerate("ab"):
+                tasks[f"O{l}{h}{letter}"] = functools.partial(outer, l, h, part)
+            tasks[f"O{l}{h}p"] = functools.partial(opm, l, h)
+            tasks[f"G{l}{h}"] = functools.partial(gate, l, h)
+            tasks[f"T{l}{h}"] = functools.partial(triangle, l, h)
+            tasks.setdefault(f"N{l}{h}", functools.partial(finish, l, h))
+    for h in range(2):
+        tasks[f"X1{h}"] = lambda h=h: stores.extend(pair_out(h))
+
+    for item in ORDER:
+        if item in tasks:
+            for name in NEEDS.get(item, ()):
+                named[name].finish()
+            tasks[item]()
+        else:
+            name, hop = item
+            named[name].event(hop)
+    for s in named.values():
         s.drain()
-    wait(stores)
+    for copy in stores:
+        copy.wait()
 
 
 def solution(mesh):

time: 296 us -> 278 us (0.939)
  Pallas kernels: 292 us -> 275 us
    pallas_call x1, Pallas kernels: 292 us -> 275 us  [device_fn(): pl.pallas_call(functools.partial(layers_kernel, chips), out_shape=jax.Sha...]
where the time goes in v4:
time: 278 us
  Pallas kernels  275 us (99%)
  local copies, waits for them, and re-layouts  3.06 us (1%)
    pallas_call x1, Pallas kernels, device_fn(): pl.pallas_call(functools.partial(layers_kernel, chips), out_shape=jax.Sha...  275 us

profile of v4, /device:TPU:21, one launch (start us, length us, event | category | flops | bytes accessed | tf_op | source)
XLA Modules:
  0.0 278.1 jit_solution(18139395822183077962)
XLA Ops:
  0.0 0.8 reshape.12
  0.8 0.6 pad_convert_fusion.b_in_ref
  1.3 274.5 %layers.1 = bf16[16,256,128]{2,1,0:T(8,128)(2,1)} custom-call(bf16[512,16,256]{2,1,0:T(8,128)(2,1)} %m_hbm.1, bf16[16,256,128]{2,1,0:T(8,128)(2,1)} %z_hbm.1, bf16[2,1024,128]{2,1,0:T(8,128)(2,1)} %wq_hbm.1, bf16[2,512,128]{2,1,0:T(8,128)(2,1)} %bitcast.4, bf16[2,128,128]{2,1,0:T(8,128)(2,1)} %wgate_hbm.1, bf16[2,128,128]{2,1,0:T(8,128)(2,1)} %wout_hbm.1, ...), custom_call_target="tpu_custom_call" | custom-call | tf_op jit(solution)/shard_map/layers/pallas_call | solution.py:522
  275.8 2.3 copy.19

commit v5 on v4

--- a/solution.py
+++ b/solution.py
@@ -152,7 +152,7 @@
         lax.fori_loop(0, dim // 8, relayout, 0)
 
 
-def triangle_half(jh, k, a_ref, b_ref, o_ref):
+def triangle_half(jh, k, add, a_ref, b_ref, o_ref):
     dim = a_ref.shape[0]
     pairs = a_ref.shape[1] // 2
 
@@ -160,8 +160,9 @@
         for u in range(8):
             c = t * 8 + u
             o = lax.dot_general(a_ref[c, :, k], b_ref[jh, c, :, k], NT, preferred_element_type=F32)
-            o_ref[0, pl.ds(c, pairs, stride=dim), :] = o[:pairs]
-            o_ref[1, pl.ds(c, pairs, stride=dim), :] = o[pairs:]
+            for e in range(2):
+                part, at = o[e * pairs : (e + 1) * pairs], pl.ds(c, pairs, stride=dim)
+                o_ref[e, at, :] = o_ref[e, at, :] + part if add else part
         return 0
 
     lax.fori_loop(0, dim // 8, step, 0)
@@ -269,21 +270,21 @@
 
 
 ORDER = (
-    "p0", ("b100", -1), ("b101", -1), "p1", ("b100", 0), ("b101", 0), ("b110", -1), ("b111", -1), "p2", ("b110", 0),
-    ("b111", 0), "p3", ("b120", -1), ("b121", -1), ("b100", 1), ("b101", 1), "vec", ("b120", 0), ("b121", 0), "w0",
-    ("b110", 1), ("b111", 1), "mask", "pin", "q0", ("b100", 2), "q1", ("b101", 2), "q2", ("b120", 1), ("b121", 1),
-    "q3", ("b110", 2), ("b111", 2), "w1", ("b100", 3), ("b101", 3), ("b120", 2), ("b121", 2), ("b110", 3),
-    ("b111", 3), ("b100", 4), ("b101", 4), ("b20", -1), ("b20", 0), ("b120", 3), ("b121", 3), ("b110", 4),
-    ("b111", 4), ("b21", -1), ("b21", 0), ("b20", 1), ("b120", 4), ("b121", 4), "O00a", "O00b", ("b21", 1), "O00p",
-    "G00", ("b20", 2), "O01a", "O01b", ("b21", 2), "O01p", "G01", ("t100", -1), ("b20", 3), ("t101", -1),
-    ("t100", 0), ("b21", 3), ("t101", 0), ("t100", 1), ("b20", 4), ("b21", 4), ("t101", 1), ("t100", 2),
-    ("t101", 2), ("t100", 3), ("t110", -1), ("t110", 0), ("t101", 3), ("t100", 4), ("t111", -1), ("t111", 0),
-    ("t110", 1), ("t101", 4), "T00", ("t111", 1), "N00", "O10a", "O10b", ("t110", 2), "O10p", "G10", ("t111", 2),
-    ("t200", -1), ("t201", -1), ("t200", 0), ("t201", 0), ("t110", 3), ("t111", 3), ("t200", 1), ("t201", 1),
-    ("t110", 4), ("t111", 4), "T01", ("t200", 2), "N01", "O11a", "O11b", ("t201", 2), "O11p", "G11", ("t210", -1),
-    ("t200", 3), ("t210", 0), ("t201", 3), ("t211", -1), ("t211", 0), ("t210", 1), ("t200", 4), ("t201", 4), "K1",
-    ("t211", 1), ("t210", 2), ("t211", 2), ("t210", 3), ("t211", 3), ("t210", 4), "T10", ("t211", 4), "N10", "X10",
-    "L1", "N11", "X11",
+    "p0", ("b100", -1), ("b101", -1), ("b100", 0), "p1", ("b101", 0), ("b110", -1), ("b110", 0), ("b111", -1), "p2",
+    ("b111", 0), ("b100", 1), ("b101", 1), "p3", ("b121", -1), ("b120", -1), "vec", ("b110", 1), "w0", "mask",
+    ("b121", 0), ("b100", 2), ("b120", 0), ("b101", 2), ("b110", 2), "pin", ("b111", 1), "q0", ("b120", 1), "q1",
+    ("b110", 3), ("b121", 1), "q2", ("b120", 2), ("b100", 3), ("b121", 2), ("b111", 2), "q3", ("b120", 3),
+    ("b20", -1), ("b110", 4), "w1", ("b100", 4), ("b101", 3), ("b20", 0), ("b111", 3), ("b21", -1), ("b21", 0),
+    ("b121", 3), ("b120", 4), "O00a", "O00b", ("b20", 1), ("b101", 4), "O00p", ("b121", 4), ("b111", 4), ("b21", 1),
+    "G00", "O01a", ("b20", 2), "O01b", ("b21", 2), "O01p", "G01", ("t100", -1), ("t110", -1), ("t100", 0),
+    ("t101", -1), ("t101", 0), ("t100", 1), ("t101", 1), ("t100", 2), ("t101", 2), ("t100", 3), ("b20", 3),
+    ("t110", 0), ("t101", 3), ("t111", -1), ("t100", 4), ("t111", 0), ("t101", 4), ("t110", 1), "T00", "N00",
+    ("b20", 4), ("t111", 1), "O10a", ("t110", 2), "O10b", ("b21", 3), "O10p", ("t111", 2), "G10", ("t200", -1),
+    ("t200", 0), ("b21", 4), ("t110", 3), ("t111", 3), ("t201", -1), ("t201", 0), ("t111", 4), ("t110", 4),
+    ("t200", 1), "T01", ("t201", 1), "N01", "O11a", ("t200", 2), "O11b", "O11p", ("t201", 2), "G11", ("t211", -1),
+    ("t200", 3), ("t210", -1), ("t210", 0), ("t211", 0), ("t200", 4), ("t201", 3), ("t210", 1), ("t211", 1),
+    ("t210", 2), ("t211", 2), ("t201", 4), "K0", ("t210", 3), "K1", ("t211", 3), ("t210", 4), "L0", ("t211", 4),
+    "N10", "X10", "L1", "N11", "X11",
 )
 NEEDS = {
     "O00a": ("b100", "b110", "b120",),
@@ -292,8 +293,9 @@
     "O10a": ("b20",),
     "T01": ("t110", "t111",),
     "O11a": ("b21",),
+    "K0": ("t200",),
     "K1": ("t201",),
-    "T10": ("t200", "t210",),
+    "L0": ("t210",),
     "L1": ("t211",),
 }
 N_STREAMS = 16
@@ -367,7 +369,9 @@
         return jnp.broadcast_to(row, (LANES, row.shape[1])).T
 
     for l in range(layers):
-        bias_ref[l] = column(b_in_ref[l])[: 2 * width]
+        for q in range(2):
+            at = pl.ds(q * width, width)
+            bias_ref[l, at, :] = column(b_in_ref[l].astype(F32)[q : q + 1])
 
     def project(l, chunk):
         def b_out(l, lanes, v):
@@ -428,8 +432,8 @@
 
         gate_half(l, h, z_ref, mask_ref, wall_ref, vec_ref, fa, fb, g_ref, a_out, b_out)
 
-    def triangle(l, jh, k=full_t, o_ref=fa):
-        triangle_half(jh, k, at_ref.at[l], t_buf.at[l], o_ref)
+    def triangle(l, jh, k=full_t, o_ref=fa, add=False):
+        triangle_half(jh, k, add, at_ref.at[l], t_buf.at[l], o_ref)
 
     def finish(l, jh, *o_refs):
         finish_half(l, jh, o_refs or (fa,), g_ref, z_ref, wo_ref, vec_ref)
@@ -465,6 +469,7 @@
         pair_in()
 
     tasks = {"vec": vectors, "mask": masks, "w0": first_weights, "w1": lambda: weights(1), "pin": first_pairs,
+             "K0": lambda: triangle(1, 0, pl.ds(0, half)), "L0": lambda: triangle(1, 0, pl.ds(half, half), add=True),
              "K1": lambda: triangle(1, 1, pl.ds(0, half), fb), "L1": lambda: triangle(1, 1, pl.ds(half, half), fa),
              "N11": lambda: finish(1, 1, fa, fb)}
     for c in range(chunks):
@@ -516,7 +521,6 @@
         z_shape = (2, pairs, dim, 2 * half)
 
         w_in = jnp.transpose(opm_w_in, (0, 2, 3, 1)).reshape(layers, 2 * width, mdim)
-        b_in = jnp.pad(opm_b_in.reshape(layers, 1, 2 * width), ((0, 0), (0, 0), (0, dim - 2 * width))).astype(F32)
         w_ab = tri_w_ab.reshape(layers, dim * 4, dim)
 
         return pl.pallas_call(
@@ -547,7 +551,7 @@
                             pltpu.SemaphoreType.DMA((N_LOADS,))],
             compiler_params=pltpu.CompilerParams(vmem_limit_bytes=VMEM_LIMIT, collective_id=0, has_side_effects=True),
             name="layers",
-        )(msa_act, pair_act, opm_w_out, w_ab, tri_w_gate, tri_w_out, w_in, b_in, opm_norm, pair_mask,
+        )(msa_act, pair_act, opm_w_out, w_ab, tri_w_gate, tri_w_out, w_in, opm_b_in, opm_norm, pair_mask,
           opm_b_out, tri_norm_in, tri_b_ab, tri_b_gate, tri_norm_out, tri_b_out)
 
     return jax.shard_map(device_fn, mesh=mesh, in_specs=(pair_spec, mask_spec, msa_spec) + (P(),) * 13,

time: 278 us -> 274 us (0.986)
  Pallas kernels: 275 us -> 272 us
    pallas_call x1, Pallas kernels: 275 us -> 272 us  [device_fn(): pl.pallas_call(functools.partial(layers_kernel, chips), out_shape=jax.Sha...]
where the time goes in v5:
time: 274 us
  Pallas kernels  272 us (99%)
    pallas_call x1, Pallas kernels, device_fn(): pl.pallas_call(functools.partial(layers_kernel, chips), out_shape=jax.Sha...  272 us

profile of v5, /device:TPU:21, one launch (start us, length us, event | category | flops | bytes accessed | tf_op | source)
XLA Modules:
  0.0 274.0 jit_solution(11890700265642026363)
XLA Ops:
  0.0 271.7 %layers.1 = bf16[16,256,128]{2,1,0:T(8,128)(2,1)} custom-call(bf16[512,16,256]{2,1,0:T(8,128)(2,1)} %m_hbm.1, bf16[16,256,128]{2,1,0:T(8,128)(2,1)} %z_hbm.1, bf16[2,1024,128]{2,1,0:T(8,128)(2,1)} %wq_hbm.1, bf16[2,512,128]{2,1,0:T(8,128)(2,1)} %bitcast.4, bf16[2,128,128]{2,1,0:T(8,128)(2,1)} %wgate_hbm.1, bf16[2,128,128]{2,1,0:T(8,128)(2,1)} %wout_hbm.1, ...), custom_call_target="tpu_custom_call" | custom-call | tf_op jit(solution)/shard_map/layers/pallas_call | solution.py:526
  271.7 2.3 copy.18

commit v6 on v5

--- a/solution.py
+++ b/solution.py
@@ -168,7 +168,7 @@
     lax.fori_loop(0, dim // 8, step, 0)
 
 
-def finish_half(l, jh, o_refs, g_ref, z_ref, wo_ref, vec_ref):
+def finish_half(l, jh, o_refs, g_ref, z_ref, wo_ref, vec_ref, store=None):
     pairs = z_ref.shape[1]
     dim = z_ref.shape[2]
 
@@ -177,7 +177,11 @@
         o = sum(jnp.concatenate([o_ref[0, at, :], o_ref[1, at, :]], axis=1) for o_ref in o_refs)
         on = norm_rows(o, twice(vec_ref[l, V_NO0]), twice(vec_ref[l, V_NO1]))
         u = jnp.dot(wo_ref[l], on, preferred_element_type=F32) + twice(vec_ref[l, V_BO])
-        z_ref[jh, p] = (z_ref[jh, p].astype(F32) + g_ref[jh, p] * u.astype(BF16).astype(F32)).astype(BF16)
+        z_new = (z_ref[jh, p].astype(F32) + g_ref[jh, p] * u.astype(BF16).astype(F32)).astype(BF16)
+        if store is None:
+            z_ref[jh, p] = z_new
+        else:
+            store(p, z_new.astype(F32))
         return 0
 
     lax.fori_loop(0, pairs, step, 0)
@@ -284,7 +288,7 @@
     ("t200", 1), "T01", ("t201", 1), "N01", "O11a", ("t200", 2), "O11b", "O11p", ("t201", 2), "G11", ("t211", -1),
     ("t200", 3), ("t210", -1), ("t210", 0), ("t211", 0), ("t200", 4), ("t201", 3), ("t210", 1), ("t211", 1),
     ("t210", 2), ("t211", 2), ("t201", 4), "K0", ("t210", 3), "K1", ("t211", 3), ("t210", 4), "L0", ("t211", 4),
-    "N10", "X10", "L1", "N11", "X11",
+    "N10", "X10", "L1", "Y11",
 )
 NEEDS = {
     "O00a": ("b100", "b110", "b120",),
@@ -299,13 +303,13 @@
     "L1": ("t211",),
 }
 N_STREAMS = 16
-N_LOADS = 32
+N_LOADS = 28
 
 
 def layers_kernel(chips, m_hbm, z_hbm, wq_hbm, wab_hbm, wgate_hbm, wout_hbm, w_in_ref, b_in_ref, opm_norm_ref, mask_in,
                   bq_ref, norm_in_ref, b_ab_ref, b_gate_ref, norm_out_ref, b_o_ref, out_hbm,
                   b_buf, t_buf, a_ref, z_ref, at_ref, g_ref, q_scr, fa, fb, b_scr, wq_ref, wall_ref, wo_ref, vec_ref,
-                  bias_ref, mask_ref, ring_send, ring_recv, core_send, core_recv, local_sem):
+                  bias_ref, mask_ref, ring_send, ring_recv, core_send, core_recv, local_sem, out_sem):
     me = lax.axis_index("dap")
     chip, core = me // 2, lax.rem(me, 2)
     rows, cols, dim = z_hbm.shape
@@ -332,17 +336,19 @@
     z_raw = t_buf.at[layers - 1, 1]
     chunks = seqs // LANES
     m_loads = [load(m_hbm.at[pl.ds(a * LANES, LANES)], m_ref.at[:, pl.ds(a * rows, rows), :]) for a in range(chunks)]
-    z_loads = [load(z_hbm.at[:, pl.ds((2 * c + h) * rows, rows), :],
-                    z_raw.at[pl.ds(0, rows), pl.ds(c * rows, rows), pl.ds(h * dim, dim)])
-               for h in range(2) for c in range(chips)]
-    w_loads = []
-    for l in range(layers):
-        cd, ab = wq_hbm.shape[1], wab_hbm.shape[1]
-        lanes = pl.ds(0, dim)
-        w_loads.append(load(wq_hbm.at[l], q_scr.at[l, :, lanes]))
-        w_loads.append(load(wab_hbm.at[l], q_scr.at[2 + l, pl.ds(0, ab), lanes]))
-        w_loads.append(load(wgate_hbm.at[l], q_scr.at[4 + l, pl.ds(0, dim), lanes]))
-        w_loads.append(load(wout_hbm.at[l], q_scr.at[4 + l, pl.ds(dim, dim), lanes]))
+    z_loads, w_loads = [], []
+
+    def later_loads():
+        z_loads.extend([load(z_hbm.at[:, pl.ds((2 * c + h) * rows, rows), :],
+                        z_raw.at[pl.ds(0, rows), pl.ds(c * rows, rows), pl.ds(h * dim, dim)])
+                   for h in range(2) for c in range(chips)])
+        for l in range(layers):
+            cd, ab = wq_hbm.shape[1], wab_hbm.shape[1]
+            lanes = pl.ds(0, dim)
+            w_loads.append(load(wq_hbm.at[l], q_scr.at[l, :, lanes]))
+            w_loads.append(load(wab_hbm.at[l], q_scr.at[2 + l, pl.ds(0, ab), lanes]))
+            w_loads.append(load(wgate_hbm.at[l], q_scr.at[4 + l, pl.ds(0, dim), lanes]))
+            w_loads.append(load(wout_hbm.at[l], q_scr.at[4 + l, pl.ds(dim, dim), lanes]))
 
     where = (chip, core, chips)
     count = [0]
@@ -438,22 +444,25 @@
     def finish(l, jh, *o_refs):
         finish_half(l, jh, o_refs or (fa,), g_ref, z_ref, wo_ref, vec_ref)
 
-    def pair_out(h):
-        def step(p, _):
+    def handed(h, p, e):
+        row = e * pairs + p
+        return pltpu.make_async_copy(at_ref.at[0, pl.ds(row * chips, chips), :, pl.ds(h * half, half)],
+                                     out_hbm.at[row, :, h], out_sem.at[h, p, e])
+
+    def last_columns(h, *o_refs):
+        def store(p, x):
             for e in range(2):
-                x = z_ref[h, p, :, e * half : (e + 1) * half].astype(F32)
-                q_scr[p, h * half : (h + 1) * half, e * dim : (e + 1) * dim] = x.T.astype(BF16)
-            return 0
-
-        lax.fori_loop(0, pairs, step, 0)
-        return [load(q_scr.at[:, pl.ds(h * half + c * rows, rows), pl.ds(e * dim, dim)],
-                     out_hbm.at[pl.ds(e * pairs, pairs), pl.ds((2 * c + h) * rows, rows), :])
-                for e in range(2) for c in range(chips)]
-
-    stores = []
+                block = x[:, e * half : (e + 1) * half].T.astype(BF16).reshape(chips, rows, dim)
+                at_ref[0, pl.ds((e * pairs + p) * chips, chips), :, h * half : (h + 1) * half] = block
+            for e in range(2):
+                handed(h, p, e).start()
+
+        finish_half(layers - 1, h, o_refs, g_ref, z_ref, wo_ref, vec_ref, store)
 
     def first_project(chunk):
         m_loads[chunk].wait()
+        if chunk == 0:
+            later_loads()
         project(0, chunk)
         if chunk == 0:
             pl.semaphore_wait(barrier, 3)
@@ -470,8 +479,8 @@
 
     tasks = {"vec": vectors, "mask": masks, "w0": first_weights, "w1": lambda: weights(1), "pin": first_pairs,
              "K0": lambda: triangle(1, 0, pl.ds(0, half)), "L0": lambda: triangle(1, 0, pl.ds(half, half), add=True),
-             "K1": lambda: triangle(1, 1, pl.ds(0, half), fb), "L1": lambda: triangle(1, 1, pl.ds(half, half), fa),
-             "N11": lambda: finish(1, 1, fa, fb)}
+             "K1": lambda: triangle(1, 1, pl.ds(0, half), fb), "N10": lambda: last_columns(0, fa), "L1": lambda: triangle(1, 1, pl.ds(half, half), fa), "Y11": lambda: last_columns(1, fa, fb),
+             "X10": lambda: None}
     for c in range(chunks):
         tasks[f"p{c}"] = functools.partial(first_project, c)
         tasks[f"q{c}"] = functools.partial(project, 1, c)
@@ -483,9 +492,6 @@
             tasks[f"G{l}{h}"] = functools.partial(gate, l, h)
             tasks[f"T{l}{h}"] = functools.partial(triangle, l, h)
             tasks.setdefault(f"N{l}{h}", functools.partial(finish, l, h))
-    for h in range(2):
-        tasks[f"X1{h}"] = lambda h=h: stores.extend(pair_out(h))
-
     for item in ORDER:
         if item in tasks:
             for name in NEEDS.get(item, ()):
@@ -496,8 +502,10 @@
             named[name].event(hop)
     for s in named.values():
         s.drain()
-    for copy in stores:
-        copy.wait()
+    for h in range(2):
+        for p in range(pairs):
+            for e in range(2):
+                handed(h, p, e).wait()
 
 
 def solution(mesh):
@@ -525,7 +533,7 @@
 
         return pl.pallas_call(
             functools.partial(layers_kernel, chips),
-            out_shape=jax.ShapeDtypeStruct(pair_act.shape, BF16),
+            out_shape=jax.ShapeDtypeStruct((rows, chips, 2, rows, dim), BF16),
             in_specs=[any_spec] * 6 + [vmem_spec] * 10,
             out_specs=any_spec,
             scratch_shapes=[pltpu.VMEM((layers, 2, width, half, seqs), BF16),
@@ -548,11 +556,12 @@
                             pltpu.SemaphoreType.DMA((N_STREAMS, 2, hops)),
                             pltpu.SemaphoreType.DMA((N_STREAMS, 2 + 2 * hops)),
                             pltpu.SemaphoreType.DMA((N_STREAMS, 2 + 2 * hops)),
-                            pltpu.SemaphoreType.DMA((N_LOADS,))],
+                            pltpu.SemaphoreType.DMA((N_LOADS,)),
+                            pltpu.SemaphoreType.DMA((2, pairs, 2))],
             compiler_params=pltpu.CompilerParams(vmem_limit_bytes=VMEM_LIMIT, collective_id=0, has_side_effects=True),
             name="layers",
         )(msa_act, pair_act, opm_w_out, w_ab, tri_w_gate, tri_w_out, w_in, opm_b_in, opm_norm, pair_mask,
-          opm_b_out, tri_norm_in, tri_b_ab, tri_b_gate, tri_norm_out, tri_b_out)
+          opm_b_out, tri_norm_in, tri_b_ab, tri_b_gate, tri_norm_out, tri_b_out).reshape(pair_act.shape)
 
     return jax.shard_map(device_fn, mesh=mesh, in_specs=(pair_spec, mask_spec, msa_spec) + (P(),) * 13,
                          out_specs=pair_spec, check_vma=False)

time: 274 us -> 274 us (level)
  no operation moved by 1% of the time
where the time goes in v6:
time: 274 us
  Pallas kernels  271 us (99%)
    pallas_call x1, Pallas kernels, device_fn(): pl.pallas_call(functools.partial(layers_kernel, chips), out_shape=jax.Sha...  271 us

profile of v6, /device:TPU:21, one launch (start us, length us, event | category | flops | bytes accessed | tf_op | source)
XLA Modules:
  0.0 273.7 jit_solution(12851314830840858164)
XLA Ops:
  0.0 271.4 %layers.1 = bf16[16,8,2,16,128]{4,3,2,1,0:T(8,128)(2,1)} custom-call(bf16[512,16,256]{2,1,0:T(8,128)(2,1)} %m_hbm.1, bf16[16,256,128]{2,1,0:T(8,128)(2,1)} %z_hbm.1, bf16[2,1024,128]{2,1,0:T(8,128)(2,1)} %wq_hbm.1, bf16[2,512,128]{2,1,0:T(8,128)(2,1)} %bitcast.6, bf16[2,128,128]{2,1,0:T(8,128)(2,1)} %wgate_hbm.1, bf16[2,128,128]{2,1,0:T(8,128)(2,1)} %wout_hbm.1, ...), custom_call_target="tpu_custom_call" | custom-call | tf_op jit(solution)/shard_map/layers/pallas_call | solution.py:534
  271.4 2.3 copy.18

commit v7 on v6

--- a/solution.py
+++ b/solution.py
@@ -152,7 +152,7 @@
         lax.fori_loop(0, dim // 8, relayout, 0)
 
 
-def triangle_half(jh, k, add, a_ref, b_ref, o_ref):
+def triangle_half(jh, k, add, groups, a_ref, b_ref, o_ref):
     dim = a_ref.shape[0]
     pairs = a_ref.shape[1] // 2
 
@@ -165,7 +165,8 @@
                 o_ref[e, at, :] = o_ref[e, at, :] + part if add else part
         return 0
 
-    lax.fori_loop(0, dim // 8, step, 0)
+    for lo, hi in groups or ((0, dim),):
+        lax.fori_loop(lo // 8, hi // 8, step, 0)
 
 
 def finish_half(l, jh, o_refs, g_ref, z_ref, wo_ref, vec_ref, store=None):
@@ -252,11 +253,15 @@
         def _():
             self.across(1, self.chip, 1 - self.core).wait_recv()
 
-        for hop in range(1, last + 1):
+        def hop_came(hop, _):
             for side in range(2):
                 origin = self.near((2 * side - 1) * hop)
-                piece = side if hop == last else None
-                self.across(2 + 2 * (hop - 1) + side, origin, 1 - self.core, piece).wait_recv()
+                self.across(2 * hop + side, origin, 1 - self.core).wait_recv()
+            return 0
+
+        lax.fori_loop(1, last, hop_came, 0)
+        for side in range(2):
+            self.across(2 * last + side, self.near(last), 1 - self.core, side).wait_recv()
 
     def drain(self):
         last = self.chips // 2
@@ -266,29 +271,35 @@
             self.across(0, self.chip, 1 - self.core).wait_send()
             self.across(1, self.chip, self.core).wait_send()
 
+        def hop_sent(hop, _):
+            for side in range(2):
+                self.ring(side, hop, self.chip).wait_send()
+                self.across(2 + 2 * hop + side, self.chip, self.core).wait_send()
+            return 0
+
+        lax.fori_loop(0, last - 1, hop_sent, 0)
         for side in range(2):
-            for hop in range(last):
-                self.ring(side, hop, self.chip, side if hop == last - 1 else None).wait_send()
-            for hop in range(1, last + 1):
-                self.across(2 + 2 * (hop - 1) + side, self.chip, self.core, side if hop == last else None).wait_send()
+            self.ring(side, last - 1, self.chip, side).wait_send()
+            self.across(2 * last + side, self.chip, self.core, side).wait_send()
 
 
 ORDER = (
-    "p0", ("b100", -1), ("b101", -1), ("b100", 0), "p1", ("b101", 0), ("b110", -1), ("b110", 0), ("b111", -1), "p2",
-    ("b111", 0), ("b100", 1), ("b101", 1), "p3", ("b121", -1), ("b120", -1), "vec", ("b110", 1), "w0", "mask",
-    ("b121", 0), ("b100", 2), ("b120", 0), ("b101", 2), ("b110", 2), "pin", ("b111", 1), "q0", ("b120", 1), "q1",
-    ("b110", 3), ("b121", 1), "q2", ("b120", 2), ("b100", 3), ("b121", 2), ("b111", 2), "q3", ("b120", 3),
-    ("b20", -1), ("b110", 4), "w1", ("b100", 4), ("b101", 3), ("b20", 0), ("b111", 3), ("b21", -1), ("b21", 0),
-    ("b121", 3), ("b120", 4), "O00a", "O00b", ("b20", 1), ("b101", 4), "O00p", ("b121", 4), ("b111", 4), ("b21", 1),
-    "G00", "O01a", ("b20", 2), "O01b", ("b21", 2), "O01p", "G01", ("t100", -1), ("t110", -1), ("t100", 0),
-    ("t101", -1), ("t101", 0), ("t100", 1), ("t101", 1), ("t100", 2), ("t101", 2), ("t100", 3), ("b20", 3),
-    ("t110", 0), ("t101", 3), ("t111", -1), ("t100", 4), ("t111", 0), ("t101", 4), ("t110", 1), "T00", "N00",
-    ("b20", 4), ("t111", 1), "O10a", ("t110", 2), "O10b", ("b21", 3), "O10p", ("t111", 2), "G10", ("t200", -1),
-    ("t200", 0), ("b21", 4), ("t110", 3), ("t111", 3), ("t201", -1), ("t201", 0), ("t111", 4), ("t110", 4),
-    ("t200", 1), "T01", ("t201", 1), "N01", "O11a", ("t200", 2), "O11b", "O11p", ("t201", 2), "G11", ("t211", -1),
-    ("t200", 3), ("t210", -1), ("t210", 0), ("t211", 0), ("t200", 4), ("t201", 3), ("t210", 1), ("t211", 1),
-    ("t210", 2), ("t211", 2), ("t201", 4), "K0", ("t210", 3), "K1", ("t211", 3), ("t210", 4), "L0", ("t211", 4),
-    "N10", "X10", "L1", "Y11",
+    "p0", ("b100", -1), ("b101", -1), ("b100", 0), "p1", ("b110", -1), ("b101", 0), ("b110", 0), ("b111", -1),
+    ("b100", 1), "p2", ("b110", 1), ("b111", 0), ("b101", 1), "p3", ("b100", 2), ("b121", -1), ("b120", -1), "vec",
+    ("b120", 0), ("b111", 1), ("b121", 0), "w0", ("b110", 2), "mask", "pin", ("b101", 2), ("b120", 1), "q0",
+    ("b100", 3), ("b110", 3), ("b121", 1), "q1", ("b100", 4), ("b120", 2), "q2", ("b111", 2), ("b121", 2), "q3",
+    ("b120", 3), ("b20", -1), ("b101", 3), ("b20", 0), ("b110", 4), ("b111", 3), ("b21", -1), ("b121", 3),
+    ("b21", 0), ("b120", 4), "w1", "O00a", ("b111", 4), "O00b", ("b20", 1), ("b101", 4), "O00p", ("b21", 1),
+    ("b121", 4), "G00", "O01a", ("b20", 2), "O01b", ("b21", 2), "O01p", "G01", ("t110", -1), ("t101", -1),
+    ("t100", -1), ("t100", 0), ("b20", 3), ("t101", 0), ("t110", 0), ("b20", 4), ("t100", 1), ("t101", 1),
+    ("t100", 2), ("t101", 2), ("t100", 3), ("t111", -1), ("t101", 3), ("t100", 4), ("t111", 0), ("t110", 1),
+    ("t101", 4), ("t111", 1), "T00", ("b21", 3), ("t110", 2), "N00", "O10a", ("t111", 2), "O10b", "O10p",
+    ("t110", 3), "G10", ("t200", -1), ("t111", 3), ("t110", 4), ("t200", 0), ("t201", -1), ("t201", 0), ("b21", 4),
+    ("t111", 4), ("t200", 1), "T01", ("t201", 1), "N01", "O11a", ("t200", 2), "O11b", "O11p", ("t201", 2), "G11",
+    ("t210", -1), ("t210", 0), ("t200", 3), ("t201", 3), ("t210", 1), ("t2111", -1), ("t2110", -1), ("t200", 4),
+    ("t2110", 0), "K0", ("t201", 4), ("t2111", 0), ("t210", 2), ("t2110", 1), ("t210", 3), ("t2111", 1), "K1",
+    ("t2110", 2), ("t210", 4), ("t2111", 2), "L0", ("t2110", 3), "N10", ("t2111", 3), ("t2110", 4), "X10",
+    ("t2111", 4), "L1a", "L1b", "Y11",
 )
 NEEDS = {
     "O00a": ("b100", "b110", "b120",),
@@ -300,9 +311,10 @@
     "K0": ("t200",),
     "K1": ("t201",),
     "L0": ("t210",),
-    "L1": ("t211",),
+    "L1a": ("t2110",),
+    "L1b": ("t2111",),
 }
-N_STREAMS = 16
+N_STREAMS = 17
 N_LOADS = 28
 
 
@@ -369,7 +381,9 @@
         named[f"b2{q}"] = stream(b_buf.at[1, q], q, (0, width // 2), full_b)
         for s in range(2):
             named[f"t1{q}{s}"] = stream(t_buf.at[0, q], q, (s * dim // 4, dim // 4), full_t)
-            named[f"t2{s}{q}"] = stream(t_buf.at[1, q], q, (0, dim // 2), pl.ds(s * half, half))
+            if (s, q) != (1, 1):
+                named[f"t2{s}{q}"] = stream(t_buf.at[1, q], q, (0, dim // 2), pl.ds(s * half, half))
+            named[f"t211{s}"] = stream(t_buf.at[1, 1], 1, (s * dim // 4, dim // 4), pl.ds(half, half)) if q else None
 
     def column(row):
         return jnp.broadcast_to(row, (LANES, row.shape[1])).T
@@ -438,8 +452,8 @@
 
         gate_half(l, h, z_ref, mask_ref, wall_ref, vec_ref, fa, fb, g_ref, a_out, b_out)
 
-    def triangle(l, jh, k=full_t, o_ref=fa, add=False):
-        triangle_half(jh, k, add, at_ref.at[l], t_buf.at[l], o_ref)
+    def triangle(l, jh, k=full_t, o_ref=fa, add=False, groups=None):
+        triangle_half(jh, k, add, groups, at_ref.at[l], t_buf.at[l], o_ref)
 
     def finish(l, jh, *o_refs):
         finish_half(l, jh, o_refs or (fa,), g_ref, z_ref, wo_ref, vec_ref)
@@ -479,8 +493,11 @@
 
     tasks = {"vec": vectors, "mask": masks, "w0": first_weights, "w1": lambda: weights(1), "pin": first_pairs,
              "K0": lambda: triangle(1, 0, pl.ds(0, half)), "L0": lambda: triangle(1, 0, pl.ds(half, half), add=True),
-             "K1": lambda: triangle(1, 1, pl.ds(0, half), fb), "N10": lambda: last_columns(0, fa), "L1": lambda: triangle(1, 1, pl.ds(half, half), fa), "Y11": lambda: last_columns(1, fa, fb),
+             "K1": lambda: triangle(1, 1, pl.ds(0, half), fb), "N10": lambda: last_columns(0, fa), "Y11": lambda: last_columns(1, fa, fb),
              "X10": lambda: None}
+    for s, letter in enumerate("ab"):
+        groups = tuple((q * dim // 2 + s * dim // 4, q * dim // 2 + (s + 1) * dim // 4) for q in range(2))
+        tasks[f"L1{letter}"] = functools.partial(triangle, 1, 1, pl.ds(half, half), fa, False, groups)
     for c in range(chunks):
         tasks[f"p{c}"] = functools.partial(first_project, c)
         tasks[f"q{c}"] = functools.partial(project, 1, c)
@@ -502,10 +519,14 @@
             named[name].event(hop)
     for s in named.values():
         s.drain()
-    for h in range(2):
-        for p in range(pairs):
+
+    def handed_over(p, _):
+        for h in range(2):
             for e in range(2):
                 handed(h, p, e).wait()
+        return 0
+
+    lax.fori_loop(0, pairs, handed_over, 0)
 
 
 def solution(mesh):

time: 274 us -> 271 us (0.989)
    pallas_call x1, Pallas kernels: 271 us -> 269 us  [device_fn(): pl.pallas_call(functools.partial(layers_kernel, chips), out_shape=jax.Sha...]
where the time goes in v7:
time: 271 us
  Pallas kernels  269 us (99%)
    pallas_call x1, Pallas kernels, device_fn(): pl.pallas_call(functools.partial(layers_kernel, chips), out_shape=jax.Sha...  269 us

profile of v7, /device:TPU:21, one launch (start us, length us, event | category | flops | bytes accessed | tf_op | source)
XLA Modules:
  0.0 270.9 jit_solution(17921689281822300921)
XLA Ops:
  0.0 268.6 %layers.1 = bf16[16,8,2,16,128]{4,3,2,1,0:T(8,128)(2,1)} custom-call(bf16[512,16,256]{2,1,0:T(8,128)(2,1)} %m_hbm.1, bf16[16,256,128]{2,1,0:T(8,128)(2,1)} %z_hbm.1, bf16[2,1024,128]{2,1,0:T(8,128)(2,1)} %wq_hbm.1, bf16[2,512,128]{2,1,0:T(8,128)(2,1)} %bitcast.6, bf16[2,128,128]{2,1,0:T(8,128)(2,1)} %wgate_hbm.1, bf16[2,128,128]{2,1,0:T(8,128)(2,1)} %wout_hbm.1, ...), custom_call_target="tpu_custom_call" | custom-call | tf_op jit(solution)/shard_map/layers/pallas_call | solution.py:555
  268.6 2.3 copy.18

commit v8 on v7

--- a/solution.py
+++ b/solution.py
@@ -284,22 +284,22 @@
 
 
 ORDER = (
-    "p0", ("b100", -1), ("b101", -1), ("b100", 0), "p1", ("b110", -1), ("b101", 0), ("b110", 0), ("b111", -1),
-    ("b100", 1), "p2", ("b110", 1), ("b111", 0), ("b101", 1), "p3", ("b100", 2), ("b121", -1), ("b120", -1), "vec",
-    ("b120", 0), ("b111", 1), ("b121", 0), "w0", ("b110", 2), "mask", "pin", ("b101", 2), ("b120", 1), "q0",
-    ("b100", 3), ("b110", 3), ("b121", 1), "q1", ("b100", 4), ("b120", 2), "q2", ("b111", 2), ("b121", 2), "q3",
-    ("b120", 3), ("b20", -1), ("b101", 3), ("b20", 0), ("b110", 4), ("b111", 3), ("b21", -1), ("b121", 3),
-    ("b21", 0), ("b120", 4), "w1", "O00a", ("b111", 4), "O00b", ("b20", 1), ("b101", 4), "O00p", ("b21", 1),
-    ("b121", 4), "G00", "O01a", ("b20", 2), "O01b", ("b21", 2), "O01p", "G01", ("t110", -1), ("t101", -1),
-    ("t100", -1), ("t100", 0), ("b20", 3), ("t101", 0), ("t110", 0), ("b20", 4), ("t100", 1), ("t101", 1),
-    ("t100", 2), ("t101", 2), ("t100", 3), ("t111", -1), ("t101", 3), ("t100", 4), ("t111", 0), ("t110", 1),
-    ("t101", 4), ("t111", 1), "T00", ("b21", 3), ("t110", 2), "N00", "O10a", ("t111", 2), "O10b", "O10p",
-    ("t110", 3), "G10", ("t200", -1), ("t111", 3), ("t110", 4), ("t200", 0), ("t201", -1), ("t201", 0), ("b21", 4),
-    ("t111", 4), ("t200", 1), "T01", ("t201", 1), "N01", "O11a", ("t200", 2), "O11b", "O11p", ("t201", 2), "G11",
-    ("t210", -1), ("t210", 0), ("t200", 3), ("t201", 3), ("t210", 1), ("t2111", -1), ("t2110", -1), ("t200", 4),
-    ("t2110", 0), "K0", ("t201", 4), ("t2111", 0), ("t210", 2), ("t2110", 1), ("t210", 3), ("t2111", 1), "K1",
-    ("t2110", 2), ("t210", 4), ("t2111", 2), "L0", ("t2110", 3), "N10", ("t2111", 3), ("t2110", 4), "X10",
-    ("t2111", 4), "L1a", "L1b", "Y11",
+    "p0", ("b101", -1), ("b100", -1), ("b100", 0), "p1", ("b110", -1), ("b110", 0), ("b101", 0), ("b111", -1),
+    ("b100", 1), "p2", ("b111", 0), ("b110", 1), ("b101", 1), "p3", ("b121", -1), ("b120", -1), "vec", ("b121", 0),
+    ("b120", 0), ("b100", 2), "w0", ("b110", 2), "mask", ("b111", 1), ("b101", 2), "pin", ("b120", 1), "q0",
+    ("b100", 3), ("b121", 1), "q1", ("b101", 3), "q2", ("b120", 2), ("b110", 3), "q3", ("b121", 2), ("b100", 4),
+    "w1", ("b111", 2), ("b120", 3), ("b20", -1), ("b20", 0), ("b121", 3), ("b21", -1), ("b120", 4), ("b110", 4),
+    ("b21", 0), ("b111", 3), "O00a", ("b20", 1), ("b121", 4), ("b101", 4), "O00b", "O00p", ("b111", 4), ("b21", 1),
+    "G00", ("b20", 2), "O01a", "O01b", ("b21", 2), "O01p", ("b20", 3), "G01", ("t100", -1), ("t101", -1),
+    ("t110", -1), ("t100", 0), ("t101", 0), ("t100", 1), ("t110", 0), ("t101", 1), ("t100", 2), ("b20", 4),
+    ("t101", 2), ("t111", -1), ("t100", 3), ("t101", 3), ("t111", 0), ("t110", 1), ("t100", 4), ("t101", 4),
+    ("t111", 1), "T00", ("t110", 2), "N00", "O10a", ("t111", 2), "O10b", "O10p", ("b21", 3), ("t110", 3), "G10",
+    ("t111", 3), ("t200", -1), ("t200", 0), ("t111", 4), ("t201", -1), ("t201", 0), ("t110", 4), ("t200", 1), "T01",
+    ("b21", 4), "N01", ("t201", 1), "O11a", ("t200", 2), "O11b", ("t201", 2), "O11p", "G11", ("t2100", -1),
+    ("t2111", -1), ("t2101", -1), ("t2100", 0), ("t2110", -1), ("t201", 3), ("t2100", 1), ("t2101", 0), ("t200", 3),
+    ("t2111", 0), ("t201", 4), ("t2100", 2), ("t2110", 0), ("t200", 4), ("t2101", 1), ("t2100", 3), ("t2110", 1),
+    "K0", ("t2101", 2), ("t2111", 1), "K1", ("t2110", 2), ("t2100", 4), ("t2101", 3), "L0a", ("t2111", 2),
+    ("t2110", 3), ("t2101", 4), ("t2111", 3), "L0b", ("t2110", 4), "N10", "X10", ("t2111", 4), "L1a", "L1b", "Y11",
 )
 NEEDS = {
     "O00a": ("b100", "b110", "b120",),
@@ -310,11 +310,12 @@
     "O11a": ("b21",),
     "K0": ("t200",),
     "K1": ("t201",),
-    "L0": ("t210",),
+    "L0a": ("t2100",),
+    "L0b": ("t2101",),
     "L1a": ("t2110",),
     "L1b": ("t2111",),
 }
-N_STREAMS = 17
+N_STREAMS = 18
 N_LOADS = 28
 
 
@@ -381,9 +382,8 @@
         named[f"b2{q}"] = stream(b_buf.at[1, q], q, (0, width // 2), full_b)
         for s in range(2):
             named[f"t1{q}{s}"] = stream(t_buf.at[0, q], q, (s * dim // 4, dim // 4), full_t)
-            if (s, q) != (1, 1):
-                named[f"t2{s}{q}"] = stream(t_buf.at[1, q], q, (0, dim // 2), pl.ds(s * half, half))
-            named[f"t211{s}"] = stream(t_buf.at[1, 1], 1, (s * dim // 4, dim // 4), pl.ds(half, half)) if q else None
+            named[f"t21{q}{s}"] = stream(t_buf.at[1, q], q, (s * dim // 4, dim // 4), pl.ds(half, half))
+        named[f"t20{q}"] = stream(t_buf.at[1, q], q, (0, dim // 2), pl.ds(0, half))
 
     def column(row):
         return jnp.broadcast_to(row, (LANES, row.shape[1])).T
@@ -492,11 +492,12 @@
         pair_in()
 
     tasks = {"vec": vectors, "mask": masks, "w0": first_weights, "w1": lambda: weights(1), "pin": first_pairs,
-             "K0": lambda: triangle(1, 0, pl.ds(0, half)), "L0": lambda: triangle(1, 0, pl.ds(half, half), add=True),
+             "K0": lambda: triangle(1, 0, pl.ds(0, half)),
              "K1": lambda: triangle(1, 1, pl.ds(0, half), fb), "N10": lambda: last_columns(0, fa), "Y11": lambda: last_columns(1, fa, fb),
              "X10": lambda: None}
     for s, letter in enumerate("ab"):
         groups = tuple((q * dim // 2 + s * dim // 4, q * dim // 2 + (s + 1) * dim // 4) for q in range(2))
+        tasks[f"L0{letter}"] = functools.partial(triangle, 1, 0, pl.ds(half, half), fa, True, groups)
         tasks[f"L1{letter}"] = functools.partial(triangle, 1, 1, pl.ds(half, half), fa, False, groups)
     for c in range(chunks):
         tasks[f"p{c}"] = functools.partial(first_project, c)

time: 271 us -> 271 us (level)
  no operation moved by 1% of the time
where the time goes in v8:
time: 271 us; the launch traced here: 270 us
  Pallas kernels  268 us (99%)
    pallas_call x1, Pallas kernels, device_fn(): pl.pallas_call(functools.partial(layers_kernel, chips), out_shape=jax.Sha...  268 us

profile of v8, /device:TPU:21, one launch (start us, length us, event | category | flops | bytes accessed | tf_op | source)
XLA Modules:
  0.0 270.4 jit_solution(3023156188838583818)
XLA Ops:
  0.0 268.1 %layers.1 = bf16[16,8,2,16,128]{4,3,2,1,0:T(8,128)(2,1)} custom-call(bf16[512,16,256]{2,1,0:T(8,128)(2,1)} %m_hbm.1, bf16[16,256,128]{2,1,0:T(8,128)(2,1)} %z_hbm.1, bf16[2,1024,128]{2,1,0:T(8,128)(2,1)} %wq_hbm.1, bf16[2,512,128]{2,1,0:T(8,128)(2,1)} %bitcast.6, bf16[2,128,128]{2,1,0:T(8,128)(2,1)} %wgate_hbm.1, bf16[2,128,128]{2,1,0:T(8,128)(2,1)} %wout_hbm.1, ...), custom_call_target="tpu_custom_call" | custom-call | tf_op jit(solution)/shard_map/layers/pallas_call | solution.py:556
  268.1 2.3 copy.18
